TPU v7x, 128 devices: a whole 4x4x4 slice. The times are simulated.
128 devices in a mesh: row: 16 (over z_hi, y, core), col: 8 (over x, z_lo).
Axes of the slice: x: 4, y: 4, z: 4 (z_hi: 2, z_lo: 2; z = z_hi * 2 + z_lo), core: 2. Of those that a mesh axis runs over, the one named last changes fastest.
Arguments:
- observed: float32 [2048, 4096], P('row', 'col'), may hold values from -6 to 6
- psf_table: bfloat16 [64, 31, 31], replicated, may hold values from 0.049804688 to 1
- psf_index: int32 [16, 32], P('row', 'col'), may hold values from 0 to 63
- start_image: float32 [2048, 4096], P('row', 'col'), may hold values from -6 to 6
- blur_dual: float32 [2048, 4096], P('row', 'col'), may hold values from -6 to 6
- tv_dual: float32 [2, 2048, 4096], P(None, 'row', 'col'), may hold values from -1.8 to 1.8
Outputs:
- restored: float32 [2048, 4096], P('row', 'col')
- blur_dual_out: float32 [2048, 4096], P('row', 'col')
Inputs may be any that keep to these rules, and one draw needn't show every extreme that they name: `psf_index`: each entry names a row of psf_table.
All inputs are finite; a program needn't handle non-finite values.
Results may differ from a plain program's by a relative error of at most 0.0003.
Values may be sent and summed in bfloat16 or wider, within the bound.
A program may use at most 128 MiB of HBM per device.

v0:
```python
import jax
import jax.numpy as jnp
from jax import lax
from jax.sharding import PartitionSpec as P

ITERS = 2


sigma_step = 0.15
tau_step = 0.6
tv_weight = 0.5
group_size = 4


def for_sending(value):

    def short(part):
        return part.astype(jnp.bfloat16) if part.dtype == jnp.float32 else part

    return jax.tree.map(short, value)


def from_behind(block, axis, distance):
    devices = range(lax.axis_size(axis))
    route = [(i - distance, i) for i in devices if i - distance in devices]
    return lax.ppermute(block, axis, route)


def extended_2(cells, sides, width):
    for axis, dim in sides:
        count = lax.axis_size(axis)
        ends = count - 1
        head = lax.slice_in_dim(cells, 0, width, axis=dim)
        tail = lax.slice_in_dim(cells, cells.shape[dim] - width, cells.shape[dim], axis=dim)
        cells = jnp.concatenate(
            [
                lax.ppermute(tail, axis, [(i, (i + 1) % count) for i in range(ends)]),
                cells,
                lax.ppermute(head, axis, [((i + 1) % count, i) for i in range(ends)]),
            ],
            axis=dim,
        )
    return cells


def make_select(kernel_size, patch_cols):
    half_width = kernel_size // 2
    column_in = jnp.arange(patch_cols + 2 * half_width, dtype=jnp.int32)[None, :, None]
    column_out = jnp.arange(patch_cols, dtype=jnp.int32)[None, None, :]
    tap_index = jnp.arange(kernel_size, dtype=jnp.int32)[:, None, None]
    return (column_in - column_out == tap_index).astype(jnp.bfloat16)


def strip_pass(strip_in, observed_s, dual_s, index_s, kern_flat, select):
    kernel_size = select.shape[0]
    patch_cols = select.shape[2]
    half_width = (select.shape[1] - patch_cols) // 2
    patch_rows, width = observed_s.shape
    group_span = group_size * patch_cols
    group_count = width // group_span
    table_size = kern_flat.shape[0]

    def one_group(spread_sum, group_id):
        pieces = jnp.stack(
            [
                strip_in[:, member * patch_cols : member * patch_cols + patch_cols + 2 * half_width]
                for member in range(group_size)
            ]
        )
        stacked = jnp.stack(
            [pieces[:, tap_row : tap_row + patch_rows, :] for tap_row in range(kernel_size)], axis=2
        )
        onehot = (index_s[:, None] == jnp.arange(table_size, dtype=jnp.int32)[None, :]).astype(
            jnp.bfloat16
        )
        kernels = jnp.dot(onehot, kern_flat, preferred_element_type=jnp.float32).astype(
            jnp.bfloat16
        )
        kernels = kernels.reshape(group_size, kernel_size, kernel_size)
        toeplitz = jnp.einsum(
            "pab,bkj->pakj", kernels, select, preferred_element_type=jnp.float32
        ).astype(jnp.bfloat16)
        blurred = jnp.einsum(
            "piak,pakj->pij", stacked, toeplitz, preferred_element_type=jnp.float32
        )
        blurred = blurred.transpose(1, 0, 2).reshape(patch_rows, group_span)
        dual_new = (dual_s + sigma_step * (blurred - observed_s)) / (1.0 + sigma_step)
        rounded = (
            dual_new.astype(jnp.bfloat16)
            .reshape(patch_rows, group_size, patch_cols)
            .transpose(1, 0, 2)
        )
        padded_dual = jnp.pad(rounded, ((0, 0), (kernel_size - 1, kernel_size - 1), (0, 0)))
        shifted = jnp.stack(
            [
                padded_dual[
                    :,
                    kernel_size
                    - 1
                    - tap_row : kernel_size
                    - 1
                    - tap_row
                    + patch_rows
                    + 2 * half_width,
                    :,
                ]
                for tap_row in range(kernel_size)
            ],
            axis=2,
        )
        spread = jnp.einsum("praj,pakj->prk", shifted, toeplitz, preferred_element_type=jnp.float32)
        merged = jnp.zeros((patch_rows + 2 * half_width, group_span + 2 * half_width), jnp.float32)
        for member in range(group_size):
            merged = merged.at[
                :, member * patch_cols : member * patch_cols + patch_cols + 2 * half_width
            ].add(spread[member])
        previous = spread_sum
        spread_sum = previous + merged
        return (spread_sum, dual_new)

    start_sum = jnp.zeros((patch_rows + 2 * half_width, width + 2 * half_width), jnp.float32)
    spread_sum, duals = lax.scan(one_group, start_sum, jnp.arange(group_count, dtype=jnp.int32))
    return (duals.transpose(1, 0, 2).reshape(patch_rows, width), spread_sum)


def fold_rows(extended, extra, half_width):
    above_rim, above_extra = (
        from_behind(extended[-half_width:].astype(jnp.bfloat16), "row", 1).astype(jnp.float32),
        from_behind(for_sending(extra), "row", 1).astype(extra.dtype),
    )
    below_rim = from_behind(extended[:half_width], "row", -1)
    middle = extended[half_width:-half_width]
    middle = middle.at[:half_width].add(above_rim)
    middle = middle.at[-half_width:].add(below_rim)
    return (middle, above_extra)


def fold_cols(extended, extra, half_width):
    left_rim, left_extra = from_behind((extended[:, -half_width:], extra), "col", 1)
    right_rim = from_behind(extended[:, :half_width], "col", -1)
    middle = extended[:, half_width:-half_width]
    middle = middle.at[:, :half_width].add(left_rim)
    middle = middle.at[:, -half_width:].add(right_rim)
    return (middle, left_extra)


def per_device(observed, psf_table, psf_index, start_image, blur_dual, tv_dual):
    kernel_size = psf_table.shape[1]
    half_width = kernel_size // 2
    tile_rows, tile_cols = observed.shape
    table_size = psf_table.shape[0]
    table = psf_table.astype(jnp.float32)
    normed = table / jnp.sum(table, axis=(1, 2), keepdims=True)
    kern_flat = normed.astype(jnp.bfloat16).reshape(table_size, kernel_size * kernel_size)
    patch_cols = tile_cols // psf_index.shape[1]
    select = make_select(kernel_size, patch_cols)
    row_place = lax.axis_index("row") * tile_rows + jnp.arange(tile_rows, dtype=jnp.int32)
    col_place = lax.axis_index("col") * tile_cols + jnp.arange(tile_cols, dtype=jnp.int32)
    keep_rows = (row_place < tile_rows * lax.axis_size("row") - 1)[:, None]
    keep_cols = (col_place < tile_cols * lax.axis_size("col") - 1)[None, :]
    restored = start_image
    extrapolated = start_image
    dual_now = blur_dual
    tv_rows = tv_dual[0]
    tv_cols = tv_dual[1]
    for step in range(ITERS):
        padded = extended_2(extrapolated, (("row", 0), ("col", 1)), half_width)
        strip_in = padded.astype(jnp.bfloat16)
        below = padded[
            half_width + 1 : half_width + 1 + tile_rows, half_width : half_width + tile_cols
        ]
        right = padded[
            half_width : half_width + tile_rows, half_width + 1 : half_width + 1 + tile_cols
        ]
        grad_rows = jnp.where(keep_rows, below - extrapolated, 0.0)
        grad_cols = jnp.where(keep_cols, right - extrapolated, 0.0)
        dual_now, spread_sum = strip_pass(
            strip_in, observed, dual_now, psf_index[0], kern_flat, select
        )
        moved_rows = tv_rows + sigma_step * grad_rows
        moved_cols = tv_cols + sigma_step * grad_cols
        shrink = jnp.maximum(
            1.0, jnp.sqrt(moved_rows * moved_rows + moved_cols * moved_cols) / tv_weight
        )
        tv_rows = moved_rows / shrink
        tv_cols = moved_cols / shrink
        masked_rows = jnp.where(keep_rows, tv_rows, 0.0)
        masked_cols = jnp.where(keep_cols, tv_cols, 0.0)
        middle, edge_col = fold_cols(spread_sum, masked_cols[:, -1:], half_width)
        adjoint, edge_row = fold_rows(middle, masked_rows[-1:], half_width)
        diverge = masked_rows - jnp.concatenate([edge_row, masked_rows[:-1]], axis=0)
        diverge = diverge + masked_cols - jnp.concatenate([edge_col, masked_cols[:, :-1]], axis=1)
        next_image = restored - tau_step * (adjoint - diverge)
        extrapolated = 2.0 * next_image - restored
        restored = next_image
    return (restored, dual_now)


def solution(mesh):
    placed = (
        P("row", "col"),
        P(),
        P("row", "col"),
        P("row", "col"),
        P("row", "col"),
        P(None, "row", "col"),
    )
    return jax.shard_map(
        per_device,
        mesh=mesh,
        in_specs=placed,
        out_specs=(P("row", "col"), P("row", "col")),
        check_vma=False,
    )
```

profile of v0, /device:TPU:27, one launch (start us, length us, event | category | flops | bytes accessed | tf_op | source)
XLA Modules:
  0.0 167.9 jit_solution(8009175019211469860)
XLA Ops:
  1.6 5.7 %collective-permute-start = (f32[15,512]{0,1:T(8,128)S(1)}, f32[15,512]{0,1:T(8,128)S(1)}, u32[]{:S(2)}, u32[]{:S(2)}) collective-permute-start(f32[15,512]{0,1:T(8,128)S(1)} %copy.248), channel_id=1, source_target_pairs={{0,8},{8,16},{16,24},{24,32},{32,40},{40,48},{48,56},{56,64},{64,7... | collective-permute-start | bytes 92168 | tf_op jit(solution)/shard_map/ppermute | solution.py:37
  7.5 1.9 %collective-permute-start.1 = (f32[15,512]{0,1:T(8,128)S(1)}, f32[15,512]{0,1:T(8,128)S(1)}, u32[]{:S(2)}, u32[]{:S(2)}) collective-permute-start(f32[15,512]{0,1:T(8,128)S(1)} %copy.249), channel_id=1, source_target_pairs={{8,0},{16,8},{24,16},{32,24},{40,32},{48,40},{56,48},{64,56},{72,6... | collective-permute-start | bytes 92168 | tf_op jit(solution)/shard_map/ppermute | solution.py:39
  9.5 1.1 convert_reduce_fusion
  10.6 1.0 fusion.17
  12.7 3.8 %convolution_convert_fusion = bf16[4,31,158,128]{3,1,2,0:T(8,128)(2,1)} fusion(s32[158,128]{1,0:T(8,128)S(1)} %iota_subtract_fusion, bf16[4,31,31,1]{2,1,0,3:T(8,128)(2,1)S(1)} %reshape.545), kind=kOutput, calls=%fused_computation.8 | convolution fusion | flops 158616832 | bytes 5104136 | tf_op jit(solution)/shard_map/while/body/eval_jaxpr/pab,bkj->pakj/dot_general | solution.py:80
  16.7 2.1 %collective-permute-done.1 = f32[15,512]{0,1:T(8,128)S(1)} collective-permute-done((f32[15,512]{0,1:T(8,128)S(1)}, f32[15,512]{0,1:T(8,128)S(1)}, u32[]{:S(2)}, u32[]{:S(2)}) %collective-permute-start.1) | collective-permute-done | bytes 30752 | tf_op jit(solution)/shard_map/ppermute | solution.py:39
  19.1 2.6 %collective-permute-start.3 = (f32[158,15]{0,1:T(8,128)S(1)}, f32[158,15]{0,1:T(8,128)S(1)}, u32[]{:S(2)}, u32[]{:S(2)}) collective-permute-start(f32[158,15]{0,1:T(8,128)S(1)} %slice.1229), channel_id=1, source_target_pairs={{1,0},{2,1},{3,2},{4,3},{5,4},{6,5},{7,6},{9,8},{10,9},{11,10},{12... | collective-permute-start | bytes 28448 | tf_op jit(solution)/shard_map/ppermute | solution.py:39
  21.8 2.7 %collective-permute-start.2 = (bf16[158,15]{0,1:T(8,128)(2,1)S(1)}, bf16[158,15]{0,1:T(8,128)(2,1)S(1)}, u32[]{:S(2)}, u32[]{:S(2)}) collective-permute-start(bf16[158,15]{0,1:T(8,128)(2,1)S(1)} %slice.1226), channel_id=1, source_target_pairs={{0,1},{1,2},{2,3},{3,4},{4,5},{5,6},{6,7},{8,9},{9,10},{10,11},{11... | collective-permute-start | bytes 14228 | tf_op jit(solution)/shard_map/ppermute | solution.py:37
  24.5 8.8 %copy.382 = bf16[4,31,158,128]{3,0,2,1:T(4,128)(2,1)} copy(bf16[4,31,158,128]{3,1,2,0:T(8,128)(2,1)} %convolution_convert_fusion) | data formatting | bytes 10031104
  40.4 1.9 %fusion.6 = f32[4,128,128,1]{1,2,3,0:T(8,128)S(1)} fusion(bf16[4,128,31,158]{1,3,2,0:T(8,128)(2,1)S(1)} %constant_dynamic-update-slice_fusion, bf16[4,31,158,128]{3,0,2,1:T(4,128)(2,1)S(1)} %copy-done), kind=kOutput, calls=%fused_computation.6 | convolution fusion | flops 641990656 | bytes 10293248 | tf_op jit(solution)/shard_map/while/body/eval_jaxpr/piak,pakj->pij/dot_general | solution.py:83
  44.3 4.0 %fusion.11 = f32[4,158,158]{1,2,0:T(8,128)S(1)} fusion(bf16[4,158,31,128]{3,1,2,0:T(8,128)(2,1)S(1)} %constant_dynamic-update-slice_fusion.31, bf16[4,31,158,128]{3,0,2,1:T(4,128)(2,1)} %copy.382), kind=kOutput, calls=%fused_computation.12 | convolution fusion | flops 792457216 | bytes 10430528 | tf_op jit(solution)/shard_map/while/body/eval_jaxpr/praj,pakj->prk/dot_general | solution.py:111
  49.7 1.2 scatter-add.59
  51.6 1.1 scatter-add.60
  52.7 3.6 %collective-permute-start.4 = (f32[158,15]{0,1:T(8,128)S(1)}, f32[158,15]{0,1:T(8,128)S(1)}, u32[]{:S(2)}, u32[]{:S(2)}) collective-permute-start(f32[158,15]{0,1:T(8,128)S(1)} %slice.1269), channel_id=1, source_target_pairs={{0,1},{1,2},{2,3},{3,4},{4,5},{5,6},{6,7},{8,9},{9,10},{10,11},{11... | collective-permute-start | bytes 28448 | tf_op jit(solution)/shard_map/ppermute | solution.py:26
  56.3 1.8 %collective-permute-done.4 = f32[158,15]{0,1:T(8,128)S(1)} collective-permute-done((f32[158,15]{0,1:T(8,128)S(1)}, f32[158,15]{0,1:T(8,128)S(1)}, u32[]{:S(2)}, u32[]{:S(2)}) %collective-permute-start.4) | collective-permute-done | bytes 9512 | tf_op jit(solution)/shard_map/ppermute | solution.py:26
  58.7 2.6 %collective-permute-start.5 = (f32[158,15]{0,1:T(8,128)S(1)}, f32[158,15]{0,1:T(8,128)S(1)}, u32[]{:S(2)}, u32[]{:S(2)}) collective-permute-start(f32[158,15]{0,1:T(8,128)S(1)} %get-tuple-element.309), channel_id=1, source_target_pairs={{1,0},{2,1},{3,2},{4,3},{5,4},{6,5},{7,6},{9,8},{10,9},{11,10},{12... | collective-permute-start | bytes 28448 | tf_op jit(solution)/shard_map/ppermute | solution.py:26
  61.9 1.3 collective-permute-done.5
  63.5 8.1 %collective-permute-start.6 = (bf16[15,512]{0,1:T(8,128)(2,1)S(1)}, bf16[15,512]{0,1:T(8,128)(2,1)S(1)}, u32[]{:S(2)}, u32[]{:S(2)}) collective-permute-start(bf16[15,512]{0,1:T(8,128)(2,1)S(1)} %slice.1883), channel_id=1, source_target_pairs={{0,8},{8,16},{16,24},{24,32},{32,40},{40,48},{48,56},{56,64},{64,7... | collective-permute-start | bytes 46088 | tf_op jit(solution)/shard_map/ppermute | solution.py:26
  71.5 1.3 broadcast_select_fusion.1
  73.0 1.9 %collective-permute-start.8 = (bf16[1,512]{0,1:T(8,128)(2,1)S(1)}, bf16[1,512]{0,1:T(8,128)(2,1)S(1)}, u32[]{:S(2)}, u32[]{:S(2)}) collective-permute-start(bf16[1,512]{0,1:T(8,128)(2,1)S(1)} %slice.1882), channel_id=1, source_target_pairs={{0,8},{8,16},{16,24},{24,32},{32,40},{40,48},{48,56},{56,64},{64,7... | collective-permute-start | bytes 3080 | tf_op jit(solution)/shard_map/ppermute | solution.py:26
  75.7 2.4 %collective-permute-start.7 = (f32[15,512]{0,1:T(8,128)}, f32[15,512]{0,1:T(8,128)S(1)}, u32[]{:S(2)}, u32[]{:S(2)}) collective-permute-start(f32[15,512]{0,1:T(8,128)} %get-tuple-element.315), channel_id=1, source_target_pairs={{8,0},{16,8},{24,16},{32,24},{40,32},{48,40},{56,48},{64,56},{72,6... | collective-permute-start | bytes 92168 | tf_op jit(solution)/shard_map/ppermute | solution.py:26
  78.2 3.5 %collective-permute-start.9 = (f32[128,1]{0,1:T(1,128)S(1)}, f32[128,1]{0,1:T(1,128)S(1)}, u32[]{:S(2)}, u32[]{:S(2)}) collective-permute-start(f32[128,1]{0,1:T(1,128)S(1)} %slice.1279), channel_id=1, source_target_pairs={{0,1},{1,2},{2,3},{3,4},{4,5},{5,6},{6,7},{8,9},{9,10},{10,11},{11... | collective-permute-start | bytes 1544 | tf_op jit(solution)/shard_map/ppermute | solution.py:26
  81.9 1.1 scatter-add.72
  83.0 4.2 %collective-permute-done.7 = f32[15,512]{0,1:T(8,128)S(1)} collective-permute-done((f32[15,512]{0,1:T(8,128)}, f32[15,512]{0,1:T(8,128)S(1)}, u32[]{:S(2)}, u32[]{:S(2)}) %collective-permute-start.7) | collective-permute-done | bytes 30752 | tf_op jit(solution)/shard_map/ppermute | solution.py:26
  87.3 1.5 scatter-add.73
  89.1 3.7 %collective-permute-start.10 = (f32[15,512]{0,1:T(8,128)S(1)}, f32[15,512]{0,1:T(8,128)S(1)}, u32[]{:S(2)}, u32[]{:S(2)}) collective-permute-start(f32[15,512]{0,1:T(8,128)S(1)} %get-tuple-element.321), channel_id=1, source_target_pairs={{0,8},{8,16},{16,24},{24,32},{32,40},{40,48},{48,56},{56,64},{64,7... | collective-permute-start | bytes 92168 | tf_op jit(solution)/shard_map/ppermute | solution.py:37
  92.9 1.9 %collective-permute-start.11 = (f32[15,512]{0,1:T(8,128)S(1)}, f32[15,512]{0,1:T(8,128)S(1)}, u32[]{:S(2)}, u32[]{:S(2)}) collective-permute-start(f32[15,512]{0,1:T(8,128)S(1)} %get-tuple-element.322), channel_id=1, source_target_pairs={{8,0},{16,8},{24,16},{32,24},{40,32},{48,40},{56,48},{64,56},{72,6... | collective-permute-start | bytes 92168 | tf_op jit(solution)/shard_map/ppermute | solution.py:39
  94.8 1.5 collective-permute-done.10
  96.3 7.9 %collective-permute-done.11 = f32[15,512]{0,1:T(8,128)S(1)} collective-permute-done((f32[15,512]{0,1:T(8,128)S(1)}, f32[15,512]{0,1:T(8,128)S(1)}, u32[]{:S(2)}, u32[]{:S(2)}) %collective-permute-start.11) | collective-permute-done | bytes 30752 | tf_op jit(solution)/shard_map/ppermute | solution.py:39
  104.4 1.9 %collective-permute-start.13 = (f32[158,15]{0,1:T(8,128)S(1)}, f32[158,15]{0,1:T(8,128)S(1)}, u32[]{:S(2)}, u32[]{:S(2)}) collective-permute-start(f32[158,15]{0,1:T(8,128)S(1)} %slice.1286), channel_id=1, source_target_pairs={{1,0},{2,1},{3,2},{4,3},{5,4},{6,5},{7,6},{9,8},{10,9},{11,10},{12... | collective-permute-start | bytes 28448 | tf_op jit(solution)/shard_map/ppermute | solution.py:39
  106.4 3.6 %collective-permute-start.12 = (bf16[158,15]{0,1:T(8,128)(2,1)S(1)}, bf16[158,15]{0,1:T(8,128)(2,1)S(1)}, u32[]{:S(2)}, u32[]{:S(2)}) collective-permute-start(bf16[158,15]{0,1:T(8,128)(2,1)S(1)} %slice.1283), channel_id=1, source_target_pairs={{0,1},{1,2},{2,3},{3,4},{4,5},{5,6},{6,7},{8,9},{9,10},{10,11},{11... | collective-permute-start | bytes 14228 | tf_op jit(solution)/shard_map/ppermute | solution.py:37
  110.0 1.7 %collective-permute-done.12 = bf16[158,15]{0,1:T(8,128)(2,1)S(1)} collective-permute-done((bf16[158,15]{0,1:T(8,128)(2,1)S(1)}, bf16[158,15]{0,1:T(8,128)(2,1)S(1)}, u32[]{:S(2)}, u32[]{:S(2)}) %collective-permute-start.12) | collective-permute-done | bytes 4772 | tf_op jit(solution)/shard_map/ppermute | solution.py:37
  116.4 1.9 %fusion = f32[4,128,128,1]{1,2,0,3:T(8,128)S(1)} fusion(bf16[4,128,31,158]{1,3,0,2:T(8,128)(2,1)S(1)} %constant_dynamic-update-slice_fusion.62, bf16[4,31,158,128]{3,0,2,1:T(4,128)(2,1)S(1)} %bitcast.854), kind=kOutput, calls=%fused_computation | convolution fusion | flops 641990656 | bytes 10293248 | tf_op jit(solution)/shard_map/while/body/eval_jaxpr/piak,pakj->pij/dot_general | solution.py:83
  120.9 4.0 %fusion.14 = f32[4,158,158]{1,2,0:T(8,128)S(1)} fusion(bf16[4,158,31,128]{3,1,2,0:T(8,128)(2,1)S(1)} %constant_dynamic-update-slice_fusion.93, bf16[4,31,158,128]{3,0,2,1:T(4,128)(2,1)} %copy.382), kind=kOutput, calls=%fused_computation.13 | convolution fusion | flops 792457216 | bytes 10430528 | tf_op jit(solution)/shard_map/while/body/eval_jaxpr/praj,pakj->prk/dot_general | solution.py:111
  126.4 1.2 scatter-add.77
  127.7 1.5 add_select_fusion
  129.2 1.1 scatter-add.78
  131.3 2.5 %collective-permute-start.14 = (f32[158,15]{0,1:T(8,128)S(1)}, f32[158,15]{0,1:T(8,128)S(1)}, u32[]{:S(2)}, u32[]{:S(2)}) collective-permute-start(f32[158,15]{0,1:T(8,128)S(1)} %slice.1326), channel_id=1, source_target_pairs={{0,1},{1,2},{2,3},{3,4},{4,5},{5,6},{6,7},{8,9},{9,10},{10,11},{11... | collective-permute-start | bytes 28448 | tf_op jit(solution)/shard_map/ppermute | solution.py:26
  133.8 2.9 %collective-permute-done.14 = f32[158,15]{0,1:T(8,128)S(1)} collective-permute-done((f32[158,15]{0,1:T(8,128)S(1)}, f32[158,15]{0,1:T(8,128)S(1)}, u32[]{:S(2)}, u32[]{:S(2)}) %collective-permute-start.14) | collective-permute-done | bytes 9512 | tf_op jit(solution)/shard_map/ppermute | solution.py:26
  137.2 1.9 %collective-permute-start.15 = (f32[158,15]{0,1:T(8,128)S(1)}, f32[158,15]{0,1:T(8,128)S(1)}, u32[]{:S(2)}, u32[]{:S(2)}) collective-permute-start(f32[158,15]{0,1:T(8,128)S(1)} %get-tuple-element.307), channel_id=1, source_target_pairs={{1,0},{2,1},{3,2},{4,3},{5,4},{6,5},{7,6},{9,8},{10,9},{11,10},{12... | collective-permute-start | bytes 28448 | tf_op jit(solution)/shard_map/ppermute | solution.py:26
  139.5 2.3 %collective-permute-done.15 = f32[158,15]{0,1:T(8,128)S(1)} collective-permute-done((f32[158,15]{0,1:T(8,128)S(1)}, f32[158,15]{0,1:T(8,128)S(1)}, u32[]{:S(2)}, u32[]{:S(2)}) %collective-permute-start.15) | collective-permute-done | bytes 9512 | tf_op jit(solution)/shard_map/ppermute | solution.py:26
  142.0 6.1 %collective-permute-start.16 = (bf16[15,512]{0,1:T(8,128)(2,1)S(1)}, bf16[15,512]{0,1:T(8,128)(2,1)S(1)}, u32[]{:S(2)}, u32[]{:S(2)}) collective-permute-start(bf16[15,512]{0,1:T(8,128)(2,1)S(1)} %slice.1881), channel_id=1, source_target_pairs={{0,8},{8,16},{16,24},{24,32},{32,40},{40,48},{48,56},{56,64},{64,7... | collective-permute-start | bytes 46088 | tf_op jit(solution)/shard_map/ppermute | solution.py:26
  148.1 1.9 %collective-permute-done.16 = bf16[15,512]{0,1:T(8,128)(2,1)S(1)} collective-permute-done((bf16[15,512]{0,1:T(8,128)(2,1)S(1)}, bf16[15,512]{0,1:T(8,128)(2,1)S(1)}, u32[]{:S(2)}, u32[]{:S(2)}) %collective-permute-start.16) | collective-permute-done | bytes 15392 | tf_op jit(solution)/shard_map/ppermute | solution.py:26
  150.7 1.9 %collective-permute-start.17 = (f32[15,512]{0,1:T(8,128)}, f32[15,512]{0,1:T(8,128)S(1)}, u32[]{:S(2)}, u32[]{:S(2)}) collective-permute-start(f32[15,512]{0,1:T(8,128)} %get-tuple-element.311), channel_id=1, source_target_pairs={{8,0},{16,8},{24,16},{32,24},{40,32},{48,40},{56,48},{64,56},{72,6... | collective-permute-start | bytes 92168 | tf_op jit(solution)/shard_map/ppermute | solution.py:26
  153.2 8.0 %collective-permute-start.18 = (bf16[1,512]{0,1:T(8,128)(2,1)S(1)}, bf16[1,512]{0,1:T(8,128)(2,1)S(1)}, u32[]{:S(2)}, u32[]{:S(2)}) collective-permute-start(bf16[1,512]{0,1:T(8,128)(2,1)S(1)} %slice.1880), channel_id=1, source_target_pairs={{0,8},{8,16},{16,24},{24,32},{32,40},{40,48},{48,56},{56,64},{64,7... | collective-permute-start | bytes 3080 | tf_op jit(solution)/shard_map/ppermute | solution.py:26
  161.2 2.0 %collective-permute-start.19 = (f32[128,1]{0,1:T(1,128)S(1)}, f32[128,1]{0,1:T(1,128)S(1)}, u32[]{:S(2)}, u32[]{:S(2)}) collective-permute-start(f32[128,1]{0,1:T(1,128)S(1)} %slice.1336), channel_id=1, source_target_pairs={{0,1},{1,2},{2,3},{3,4},{4,5},{5,6},{6,7},{8,9},{9,10},{10,11},{11... | collective-permute-start | bytes 1544 | tf_op jit(solution)/shard_map/ppermute | solution.py:26
  164.2 1.1 scatter-add.84
  165.4 1.5 scatter-add.87
  (237 shorter events, 30.8 us)
Async XLA Ops:
  0.6 15.9 %copy-start.7 = (f32[128,512]{1,0:T(8,128)S(1)}, f32[128,512]{1,0:T(8,128)}, u32[]{:S(2)}) copy-start(f32[128,512]{1,0:T(8,128)} %param.41) | copy-start | bytes 786436
  0.6 15.9 %copy-start.6 = (f32[2,128,512]{2,1,0:T(8,128)S(1)}, f32[2,128,512]{2,1,0:T(8,128)}, u32[]{:S(2)}) copy-start(f32[2,128,512]{2,1,0:T(8,128)} %param.43) | copy-start | bytes 1572868
  1.6 15.0 %collective-permute-start = (f32[15,512]{0,1:T(8,128)S(1)}, f32[15,512]{0,1:T(8,128)S(1)}, u32[]{:S(2)}, u32[]{:S(2)}) collective-permute-start(f32[15,512]{0,1:T(8,128)S(1)} %copy.248), channel_id=1, source_target_pairs={{0,8},{8,16},{16,24},{24,32},{32,40},{40,48},{48,56},{56,64},{64,7... | collective-permute-start | bytes 92168 | tf_op jit(solution)/shard_map/ppermute | solution.py:37
  7.5 11.3 %collective-permute-start.1 = (f32[15,512]{0,1:T(8,128)S(1)}, f32[15,512]{0,1:T(8,128)S(1)}, u32[]{:S(2)}, u32[]{:S(2)}) collective-permute-start(f32[15,512]{0,1:T(8,128)S(1)} %copy.249), channel_id=1, source_target_pairs={{8,0},{16,8},{24,16},{32,24},{40,32},{48,40},{56,48},{64,56},{72,6... | collective-permute-start | bytes 92168 | tf_op jit(solution)/shard_map/ppermute | solution.py:39
  18.8 5.6 %copy-start.4 = (f32[15,512]{0,1:T(8,128)}, f32[15,512]{0,1:T(8,128)S(1)}, u32[]{:S(2)}) copy-start(f32[15,512]{0,1:T(8,128)S(1)} %collective-permute-done.1) | copy-start | bytes 92164
  19.1 16.6 %collective-permute-start.3 = (f32[158,15]{0,1:T(8,128)S(1)}, f32[158,15]{0,1:T(8,128)S(1)}, u32[]{:S(2)}, u32[]{:S(2)}) collective-permute-start(f32[158,15]{0,1:T(8,128)S(1)} %slice.1229), channel_id=1, source_target_pairs={{1,0},{2,1},{3,2},{4,3},{5,4},{6,5},{7,6},{9,8},{10,9},{11,10},{12... | collective-permute-start | bytes 28448 | tf_op jit(solution)/shard_map/ppermute | solution.py:39
  21.8 14.0 %collective-permute-start.2 = (bf16[158,15]{0,1:T(8,128)(2,1)S(1)}, bf16[158,15]{0,1:T(8,128)(2,1)S(1)}, u32[]{:S(2)}, u32[]{:S(2)}) collective-permute-start(bf16[158,15]{0,1:T(8,128)(2,1)S(1)} %slice.1226), channel_id=1, source_target_pairs={{0,1},{1,2},{2,3},{3,4},{4,5},{5,6},{6,7},{8,9},{9,10},{10,11},{11... | collective-permute-start | bytes 14228 | tf_op jit(solution)/shard_map/ppermute | solution.py:37
  24.5 8.8 %copy-start.8 = (f32[128,512]{1,0:T(8,128)S(1)}, f32[128,512]{1,0:T(8,128)}, u32[]{:S(2)}) copy-start(f32[128,512]{1,0:T(8,128)} %param.38) | copy-start | bytes 786436
  24.5 8.9 %copy-start.9 = (f32[128,512]{1,0:T(8,128)S(1)}, f32[128,512]{1,0:T(8,128)}, u32[]{:S(2)}) copy-start(f32[128,512]{1,0:T(8,128)} %param.42) | copy-start | bytes 786436
  36.0 4.5 %copy-start = (bf16[4,31,158,128]{3,0,2,1:T(4,128)(2,1)S(1)}, bf16[4,31,158,128]{3,0,2,1:T(4,128)(2,1)}, u32[]{:S(2)}) copy-start(bf16[4,31,158,128]{3,0,2,1:T(4,128)(2,1)} %copy.382) | copy-start | bytes 15046660
  42.4 1.9 %copy-start.1 = (f32[4,128,128,1]{1,2,3,0:T(8,128)}, f32[4,128,128,1]{1,2,3,0:T(8,128)S(1)}, u32[]{:S(2)}) copy-start(f32[4,128,128,1]{1,2,3,0:T(8,128)S(1)} %fusion.6) | copy-start | bytes 786436
  52.7 5.4 %collective-permute-start.4 = (f32[158,15]{0,1:T(8,128)S(1)}, f32[158,15]{0,1:T(8,128)S(1)}, u32[]{:S(2)}, u32[]{:S(2)}) collective-permute-start(f32[158,15]{0,1:T(8,128)S(1)} %slice.1269), channel_id=1, source_target_pairs={{0,1},{1,2},{2,3},{3,4},{4,5},{5,6},{6,7},{8,9},{9,10},{10,11},{11... | collective-permute-start | bytes 28448 | tf_op jit(solution)/shard_map/ppermute | solution.py:26
  58.7 4.5 %collective-permute-start.5 = (f32[158,15]{0,1:T(8,128)S(1)}, f32[158,15]{0,1:T(8,128)S(1)}, u32[]{:S(2)}, u32[]{:S(2)}) collective-permute-start(f32[158,15]{0,1:T(8,128)S(1)} %get-tuple-element.309), channel_id=1, source_target_pairs={{1,0},{2,1},{3,2},{4,3},{5,4},{6,5},{7,6},{9,8},{10,9},{11,10},{12... | collective-permute-start | bytes 28448 | tf_op jit(solution)/shard_map/ppermute | solution.py:26
  63.5 11.4 %collective-permute-start.6 = (bf16[15,512]{0,1:T(8,128)(2,1)S(1)}, bf16[15,512]{0,1:T(8,128)(2,1)S(1)}, u32[]{:S(2)}, u32[]{:S(2)}) collective-permute-start(bf16[15,512]{0,1:T(8,128)(2,1)S(1)} %slice.1883), channel_id=1, source_target_pairs={{0,8},{8,16},{16,24},{24,32},{32,40},{40,48},{48,56},{56,64},{64,7... | collective-permute-start | bytes 46088 | tf_op jit(solution)/shard_map/ppermute | solution.py:26
  73.0 8.8 %collective-permute-start.8 = (bf16[1,512]{0,1:T(8,128)(2,1)S(1)}, bf16[1,512]{0,1:T(8,128)(2,1)S(1)}, u32[]{:S(2)}, u32[]{:S(2)}) collective-permute-start(bf16[1,512]{0,1:T(8,128)(2,1)S(1)} %slice.1882), channel_id=1, source_target_pairs={{0,8},{8,16},{16,24},{24,32},{32,40},{40,48},{48,56},{56,64},{64,7... | collective-permute-start | bytes 3080 | tf_op jit(solution)/shard_map/ppermute | solution.py:26
  75.7 11.5 %collective-permute-start.7 = (f32[15,512]{0,1:T(8,128)}, f32[15,512]{0,1:T(8,128)S(1)}, u32[]{:S(2)}, u32[]{:S(2)}) collective-permute-start(f32[15,512]{0,1:T(8,128)} %get-tuple-element.315), channel_id=1, source_target_pairs={{8,0},{16,8},{24,16},{32,24},{40,32},{48,40},{56,48},{64,56},{72,6... | collective-permute-start | bytes 92168 | tf_op jit(solution)/shard_map/ppermute | solution.py:26
  78.2 10.5 %collective-permute-start.9 = (f32[128,1]{0,1:T(1,128)S(1)}, f32[128,1]{0,1:T(1,128)S(1)}, u32[]{:S(2)}, u32[]{:S(2)}) collective-permute-start(f32[128,1]{0,1:T(1,128)S(1)} %slice.1279), channel_id=1, source_target_pairs={{0,1},{1,2},{2,3},{3,4},{4,5},{5,6},{6,7},{8,9},{9,10},{10,11},{11... | collective-permute-start | bytes 1544 | tf_op jit(solution)/shard_map/ppermute | solution.py:26
  88.8 27.5 %slice-start = ((s8[5015552]{0:T(1024)(128)(4,1)}), s8[4194304]{0:T(1024)(128)(4,1)S(1)}, s32[]{:S(2)}) async-start(s8[5015552]{0:T(1024)(128)(4,1)} %bitcast.853), calls=%async_computation | async-start | bytes 8388608
  89.1 7.2 %collective-permute-start.10 = (f32[15,512]{0,1:T(8,128)S(1)}, f32[15,512]{0,1:T(8,128)S(1)}, u32[]{:S(2)}, u32[]{:S(2)}) collective-permute-start(f32[15,512]{0,1:T(8,128)S(1)} %get-tuple-element.321), channel_id=1, source_target_pairs={{0,8},{8,16},{16,24},{24,32},{32,40},{40,48},{48,56},{56,64},{64,7... | collective-permute-start | bytes 92168 | tf_op jit(solution)/shard_map/ppermute | solution.py:37
  92.9 11.3 %collective-permute-start.11 = (f32[15,512]{0,1:T(8,128)S(1)}, f32[15,512]{0,1:T(8,128)S(1)}, u32[]{:S(2)}, u32[]{:S(2)}) collective-permute-start(f32[15,512]{0,1:T(8,128)S(1)} %get-tuple-element.322), channel_id=1, source_target_pairs={{8,0},{16,8},{24,16},{32,24},{40,32},{48,40},{56,48},{64,56},{72,6... | collective-permute-start | bytes 92168 | tf_op jit(solution)/shard_map/ppermute | solution.py:39
  104.4 5.5 %collective-permute-start.13 = (f32[158,15]{0,1:T(8,128)S(1)}, f32[158,15]{0,1:T(8,128)S(1)}, u32[]{:S(2)}, u32[]{:S(2)}) collective-permute-start(f32[158,15]{0,1:T(8,128)S(1)} %slice.1286), channel_id=1, source_target_pairs={{1,0},{2,1},{3,2},{4,3},{5,4},{6,5},{7,6},{9,8},{10,9},{11,10},{12... | collective-permute-start | bytes 28448 | tf_op jit(solution)/shard_map/ppermute | solution.py:39
  106.4 5.3 %collective-permute-start.12 = (bf16[158,15]{0,1:T(8,128)(2,1)S(1)}, bf16[158,15]{0,1:T(8,128)(2,1)S(1)}, u32[]{:S(2)}, u32[]{:S(2)}) collective-permute-start(bf16[158,15]{0,1:T(8,128)(2,1)S(1)} %slice.1283), channel_id=1, source_target_pairs={{0,1},{1,2},{2,3},{3,4},{4,5},{5,6},{6,7},{8,9},{9,10},{10,11},{11... | collective-permute-start | bytes 14228 | tf_op jit(solution)/shard_map/ppermute | solution.py:37
  112.5 3.8 %slice-start.1 = ((s8[5015552]{0:T(1024)(128)(4,1)}), s8[821248]{0:T(1024)(128)(4,1)S(1)}, s32[]{:S(2)}) async-start(s8[5015552]{0:T(1024)(128)(4,1)} %bitcast.853), calls=%async_computation.1 | async-start | bytes 1642496
  116.3 1.9 %copy-start.2 = (f32[4,128,128,1]{1,2,3,0:T(8,128)S(1)}, f32[4,128,128,1]{1,2,3,0:T(8,128)}, u32[]{:S(2)}) copy-start(f32[4,128,128,1]{1,2,3,0:T(8,128)} %copy-done.1) | copy-start | bytes 786436
  124.9 1.5 copy-start.5
  124.9 38.3 %copy-start.3 = (f32[128,512]{0,1:T(8,128)S(1)}, f32[128,512]{0,1:T(8,128)}, u32[]{:S(2)}) copy-start(f32[128,512]{0,1:T(8,128)} %get-tuple-element.295) | copy-start | bytes 786436
  131.3 5.4 %collective-permute-start.14 = (f32[158,15]{0,1:T(8,128)S(1)}, f32[158,15]{0,1:T(8,128)S(1)}, u32[]{:S(2)}, u32[]{:S(2)}) collective-permute-start(f32[158,15]{0,1:T(8,128)S(1)} %slice.1326), channel_id=1, source_target_pairs={{0,1},{1,2},{2,3},{3,4},{4,5},{5,6},{6,7},{8,9},{9,10},{10,11},{11... | collective-permute-start | bytes 28448 | tf_op jit(solution)/shard_map/ppermute | solution.py:26
  137.2 4.5 %collective-permute-start.15 = (f32[158,15]{0,1:T(8,128)S(1)}, f32[158,15]{0,1:T(8,128)S(1)}, u32[]{:S(2)}, u32[]{:S(2)}) collective-permute-start(f32[158,15]{0,1:T(8,128)S(1)} %get-tuple-element.307), channel_id=1, source_target_pairs={{1,0},{2,1},{3,2},{4,3},{5,4},{6,5},{7,6},{9,8},{10,9},{11,10},{12... | collective-permute-start | bytes 28448 | tf_op jit(solution)/shard_map/ppermute | solution.py:26
  142.0 8.0 %collective-permute-start.16 = (bf16[15,512]{0,1:T(8,128)(2,1)S(1)}, bf16[15,512]{0,1:T(8,128)(2,1)S(1)}, u32[]{:S(2)}, u32[]{:S(2)}) collective-permute-start(bf16[15,512]{0,1:T(8,128)(2,1)S(1)} %slice.1881), channel_id=1, source_target_pairs={{0,8},{8,16},{16,24},{24,32},{32,40},{40,48},{48,56},{56,64},{64,7... | collective-permute-start | bytes 46088 | tf_op jit(solution)/shard_map/ppermute | solution.py:26
  150.7 14.5 %collective-permute-start.17 = (f32[15,512]{0,1:T(8,128)}, f32[15,512]{0,1:T(8,128)S(1)}, u32[]{:S(2)}, u32[]{:S(2)}) collective-permute-start(f32[15,512]{0,1:T(8,128)} %get-tuple-element.311), channel_id=1, source_target_pairs={{8,0},{16,8},{24,16},{32,24},{40,32},{48,40},{56,48},{64,56},{72,6... | collective-permute-start | bytes 92168 | tf_op jit(solution)/shard_map/ppermute | solution.py:26
  153.2 10.8 %collective-permute-start.18 = (bf16[1,512]{0,1:T(8,128)(2,1)S(1)}, bf16[1,512]{0,1:T(8,128)(2,1)S(1)}, u32[]{:S(2)}, u32[]{:S(2)}) collective-permute-start(bf16[1,512]{0,1:T(8,128)(2,1)S(1)} %slice.1880), channel_id=1, source_target_pairs={{0,8},{8,16},{16,24},{24,32},{32,40},{40,48},{48,56},{56,64},{64,7... | collective-permute-start | bytes 3080 | tf_op jit(solution)/shard_map/ppermute | solution.py:26
  161.2 5.7 %collective-permute-start.19 = (f32[128,1]{0,1:T(1,128)S(1)}, f32[128,1]{0,1:T(1,128)S(1)}, u32[]{:S(2)}, u32[]{:S(2)}) collective-permute-start(f32[128,1]{0,1:T(1,128)S(1)} %slice.1336), channel_id=1, source_target_pairs={{0,1},{1,2},{2,3},{3,4},{4,5},{5,6},{6,7},{8,9},{9,10},{10,11},{11... | collective-permute-start | bytes 1544 | tf_op jit(solution)/shard_map/ppermute | solution.py:26
where the time goes:
time: 170 us; the launch traced here: 168 us
  starting transfers between devices  68.4 us (40%)
  local copies, waits for them, and re-layouts  36 us (21%)
  waiting for transfers between devices  27.6 us (16%)
  other arithmetic  17.3 us (10%)
  matrix products  16.5 us (10%)
  between operations  2.15 us (1%)
    ppermute x12, starting transfers between devices, from_behind(): return lax.ppermute(block, axis, route)  44.3 us
    unnamed x152, local copies, waits for them, and re-layouts  22.4 us
    ppermute x4, starting transfers between devices, extended_2(): lax.ppermute(tail, axis, [(i, (i + 1) % count) for i in range(ends)])  15.7 us
    ppermute x12, waiting for transfers between devices, from_behind(): return lax.ppermute(block, axis, route)  14.4 us
    ppermute x4, waiting for transfers between devices, extended_2(): lax.ppermute(head, axis, [((i + 1) % count, i) for i in range(ends)])  10 us
    ppermute x4, starting transfers between devices, extended_2(): lax.ppermute(head, axis, [((i + 1) % count, i) for i in range(ends)])  8.38 us
    dot_general x2, matrix products, one_group(): jnp.einsum('praj,pakj->prk', shifted, toeplitz, preferred_element_type=jn...  7.94 us
    another operation x13, other arithmetic  7.76 us
  transfers between devices with their start and end apart: 20, of which 10 were waited for; matrix products, arithmetic and copies ran while one was open for 17% of the time, Pallas kernels for 0%

commit v1 on v0

v1 whole, which is shorter than its diff:
```python
import jax
import jax.numpy as jnp
from jax import lax
from jax.experimental import pallas as pl
from jax.experimental.pallas import tpu as pltpu
from jax.sharding import PartitionSpec as P

ITERS = 2
SIGMA = 0.15
TAU = 0.6
WEIGHT = 0.5
TAPS = 31
PAIRS = 64
TILES = 4
DIRS = ((-1, 0), (1, 0), (0, -1), (0, 1), (-1, -1), (-1, 1), (1, -1), (1, 1))
MESH_ID = pl.DeviceIdType.MESH
F32 = jnp.float32
BF16 = jnp.bfloat16


def lanes(shape):
    return lax.broadcasted_iota(jnp.int32, shape, 1)


def roll(value, shift):
    shift = shift % 128
    return value if shift == 0 else pltpu.roll(value, shift, 1)


def kernel(
    index_ref, observed_hbm, table_hbm, start_hbm, dual_hbm, tv_hbm,
    restored_hbm, dual_out_hbm,
    start_v, table_v, observed_v, dual_v, tv_v, out_v,
    kern_v, base_v, weights, x_v, bar_v, obs_v, y_v, q1_v, q2_v, shifted, ypad, spread, acc,
    row_out, col_out, cor_out, row_in, col_in, cor_in,
    load_sem, store_sem, send_sem, recv_sem,
):
    row, col = lax.axis_index("row"), lax.axis_index("col")
    rows, cols = lax.axis_size("row"), lax.axis_size("col")

    def at(direction):
        dr, dc = direction
        return (lax.rem(row + dr + rows, rows), lax.rem(col + dc + cols, cols))

    barrier = pltpu.get_barrier_semaphore()
    for direction in DIRS:
        pl.semaphore_signal(barrier, inc=1, device_id=at(direction), device_id_type=MESH_ID)

    slices = [slice(128 * p, 128 * p + 128) for p in range(TILES)]
    plain = ((start_hbm, start_v), (observed_hbm, observed_v), (dual_hbm, dual_v))
    sources = [(src.at[:, slices[p]], dst.at[p]) for src, dst in plain for p in range(TILES)]
    sources += [(tv_hbm.at[:, :, slices[p]], tv_v.at[:, p]) for p in range(TILES)]
    sources.insert(TILES, (table_hbm, table_v))
    loads = [pltpu.make_async_copy(src, dst, load_sem.at[i]) for i, (src, dst) in enumerate(sources)]
    for load in loads:
        load.start()

    top, bottom = row == 0, row == rows - 1
    left, right = col == 0, col == cols - 1
    outside = (top, bottom, left, right, top | left, top | right, bottom | left, bottom | right)
    lane64 = lanes((PAIRS, 128))
    lane8 = lanes((8, 128))
    lane16 = lanes((16, 128))
    sub64 = lax.broadcasted_iota(jnp.int32, (PAIRS, 128), 0)

    def copies(exchange):
        result = []
        for d, direction in enumerate(DIRS):
            if d < 2:
                src, dst = row_out.at[exchange, d], row_in.at[exchange, d ^ 1]
            elif d < 4:
                src, dst = col_out.at[exchange, d - 2], col_in.at[exchange, (d - 2) ^ 1]
            else:
                src, dst = cor_out.at[exchange, d - 4], cor_in.at[exchange, 3 - (d - 4)]
            back = d ^ 1 if d < 4 else 4 + 3 - (d - 4)
            result.append(
                pltpu.make_async_remote_copy(
                    src_ref=src,
                    dst_ref=dst,
                    send_sem=send_sem.at[exchange, d],
                    recv_sem=recv_sem.at[exchange, back],
                    device_id=at(direction),
                    device_id_type=MESH_ID,
                )
            )
        return result

    def wait_in(exchange):
        for copy in copies(exchange):
            copy.wait()

    def packed(parts, first_lane, height):
        lane = lane16 if height == 16 else lane8
        message = None
        for f, part in enumerate(parts):
            moved = roll(part, 16 * f - first_lane)
            message = moved if f == 0 else jnp.where(lane >= 16 * f, moved, message)
        return message

    def unpacked(message, f, first_lane):
        return roll(message, first_lane - 16 * f)

    for load in loads[:TILES]:
        load.wait()
    for par in (0, 1):
        for p in range(TILES):
            value = start_v[p, pl.ds(par, PAIRS, stride=2), :]
            x_v[par, p] = value
            bar_v[par, p] = value

    def send_image(exchange):
        for d, first in ((0, 0), (1, PAIRS - 8)):
            for par in (0, 1):
                for p in range(TILES):
                    row_out[exchange, d, par, p] = bar_v[par, p, first : first + 8]
        for s, (p, first_lane) in enumerate(((0, 0), (TILES - 1, 112))):
            col_out[exchange, s] = packed(
                [bar_v[par, p, 16 * k : 16 * k + 16] for par in (0, 1) for k in range(4)], first_lane, 16
            )
            for d, first in ((0, 0), (1, PAIRS - 8)):
                cor_out[exchange, 2 * d + s] = packed(
                    [bar_v[par, p, first : first + 8] for par in (0, 1)], first_lane, 8
                )
        for copy in copies(exchange):
            copy.start()

    pl.semaphore_wait(barrier, len(DIRS))
    send_image(0)

    kern_v[...] = jnp.zeros_like(kern_v)
    loads[TILES].wait()
    for p in range(TILES):
        table = table_v[index_ref[0, p]].astype(F32)
        kern_v[8 + 32 * p : 8 + 32 * p + TAPS, 0:TAPS] = table / jnp.sum(table)
    tap = lax.broadcasted_iota(jnp.int32, (128, 128), 0)
    place = lanes((128, 128))
    flip_low = ((tap < TAPS) & (place == lax.rem(128 - tap, 128))).astype(F32).astype(BF16)
    flip_high = ((tap < TAPS) & (place == 64 - tap)).astype(F32).astype(BF16)
    base_v[...] = jnp.dot(kern_v[8:136].astype(BF16), flip_low, preferred_element_type=F32) + jnp.dot(
        kern_v[7:135].astype(BF16), flip_high, preferred_element_type=F32
    )
    reach = tap - (place & 63)
    band = (reach >= 0) & (reach < TAPS)

    unroll = 4

    def build(step, carry):
        for u in range(unroll):
            r = step * unroll + u
            line = jnp.broadcast_to(base_v[pl.ds(r, 1), :], (128, 128))
            rolled = pltpu.roll(line, 0, 1, stride=1, stride_axis=0)
            weights[pl.ds(pl.multiple_of(r * 128, 128), 128), :] = jnp.where(band, rolled, 0.0).astype(BF16)
        return carry

    lax.fori_loop(0, 128 // unroll, build, 0)

    ypad[...] = jnp.zeros_like(ypad)
    for load in loads[TILES + 1 :]:
        load.wait()
    for par in (0, 1):
        for p in range(TILES):
            rows_of = pl.ds(par, PAIRS, stride=2)
            obs_v[par, p] = observed_v[p, rows_of, :]
            y_v[par, p] = dual_v[p, rows_of, :]
            q1_v[par, p] = tv_v[0, p, rows_of, :]
            q2_v[par, p] = tv_v[1, p, rows_of, :]

    for step in range(ITERS):
        halo, fold = 2 * step, 2 * step + 1
        wait_in(halo)
        rows_in = [
            [
                [jnp.where(outside[d], 0.0, row_in[halo, d, par, p]) for p in range(TILES)]
                for par in (0, 1)
            ]
            for d in (0, 1)
        ]
        cols_in = [jnp.where(outside[2 + s], 0.0, col_in[halo, s]) for s in (0, 1)]
        cors_in = [jnp.where(outside[4 + s], 0.0, cor_in[halo, s]) for s in range(4)]

        def sides(par, first_lanes):
            return [
                jnp.concatenate(
                    [unpacked(cols_in[s], 4 * par + k, first_lanes[s]) for k in range(4)], axis=0
                )
                for s in (0, 1)
            ]

        def lay(tiles, par, first, count):
            lane = lanes((count, 128))
            by15 = [roll(t, 15) for t in tiles[:-1]]
            by79 = [roll(t, 79) for t in tiles[1:]]
            for p in range(TILES):
                shifted[par, 0, p, first : first + count] = jnp.where(lane < 15, by15[p], by15[p + 1])
                shifted[par, 1, p, first : first + count] = jnp.where(lane < 79, by79[p], by79[p + 1])

        side_tiles = [sides(par, (112, 0)) for par in (0, 1)]
        for par in (0, 1):
            lay(
                [side_tiles[par][0]] + [bar_v[par, p] for p in range(TILES)] + [side_tiles[par][1]], par, 8, PAIRS
            )
            for d, first in ((0, 0), (1, 72)):
                lay(
                    [unpacked(cors_in[2 * d], par, 112)]
                    + rows_in[d][par]
                    + [unpacked(cors_in[2 * d + 1], par, 0)],
                    par,
                    first,
                    8,
                )

        def blur(p, carry):
            pieces = []
            for t in range(16):
                pieces.append(
                    jnp.concatenate([shifted[0 + 1, h, p, t : t + PAIRS] for h in (0, 1)], axis=0).astype(BF16)
                )
                pieces.append(
                    jnp.concatenate([shifted[0, h, p, t + 1 : t + 1 + PAIRS] for h in (0, 1)], axis=0).astype(BF16)
                )
            stacked = jnp.concatenate(pieces, axis=1)
            matrix = weights[pl.ds(pl.multiple_of(p * 4096, 4096), 4096), :]
            blurred = jnp.dot(stacked, matrix, preferred_element_type=F32)
            first, second = blurred[:PAIRS], blurred[PAIRS:]
            even = jnp.where(lane64 < 64, first, roll(second, 64))
            odd = jnp.where(lane64 < 64, roll(first, 64), second)
            new = []
            for par, value in ((0, even), (1, odd)):
                updated = (y_v[par, p] + SIGMA * (value - obs_v[par, p])) / (1.0 + SIGMA)
                y_v[par, p] = updated
                new.append(updated)
            ypad[0, p, 16 : 16 + PAIRS] = jnp.where(lane64 < 64, new[0], roll(new[1], 64))
            ypad[1, p, 16 : 16 + PAIRS] = jnp.where(lane64 < 64, roll(new[0], 64), new[1])
            return carry

        lax.fori_loop(0, TILES, blur, 0)

        for p in range(TILES):
            even, odd = bar_v[0, p], bar_v[1, p]
            below = jnp.concatenate([even[1:], rows_in[1][0][p][:1]], axis=0)
            grad_even = odd - even
            grad_odd = jnp.where((sub64 == PAIRS - 1) & bottom, 0.0, below - odd)
            for par, value, grad1 in ((0, even, grad_even), (1, odd, grad_odd)):
                beyond = bar_v[par, p + 1] if p + 1 < TILES else side_tiles[par][1]
                after = jnp.where(lane64 < 127, roll(value, 127), roll(beyond, 127))
                grad2 = after - value
                if p + 1 == TILES:
                    grad2 = jnp.where((lane64 == 127) & right, 0.0, grad2)
                u1 = q1_v[par, p] + SIGMA * grad1
                u2 = q2_v[par, p] + SIGMA * grad2
                shrink = jnp.maximum(1.0, jnp.sqrt(u1 * u1 + u2 * u2) / WEIGHT)
                q1_v[par, p] = u1 / shrink
                q2_v[par, p] = u2 / shrink

        def adjoint(p, carry):
            pieces = [
                jnp.concatenate([ypad[h, p, 16 - t : 96 - t] for h in (0, 1)], axis=0).astype(BF16)
                for t in range(16)
            ]
            stacked = jnp.concatenate(pieces, axis=1)
            start = pl.multiple_of(p * 4096, 4096)
            matrix = jnp.concatenate(
                [weights[pl.ds(start + 256 * t, 256), :] for t in range(16)], axis=1
            )
            out = lax.dot_general(stacked, matrix, (((1,), (1,)), ((), ())), preferred_element_type=F32)
            for h in (0, 1):
                spread[1, h, p, 0:80] = out[80 * h : 80 * h + 80, 0:128]
                spread[0, h, p, 1:81] = out[80 * h : 80 * h + 80, 128:256]
            return carry

        lax.fori_loop(0, TILES, adjoint, 0)
        lane80 = lanes((80, 128))
        sub80 = lax.broadcasted_iota(jnp.int32, (80, 128), 0)
        for par in (0, 1):
            halves = [roll(spread[par, 1, p, 0:80], 64) for p in range(TILES)]
            total = []
            for q in range(TILES + 1):
                if q == 0:
                    value = spread[par, 0, 0, 0:80] + jnp.where(lane80 >= 64, halves[0], 0.0)
                elif q == TILES:
                    value = jnp.where(lane80 < 64, halves[q - 1], 0.0)
                else:
                    value = spread[par, 0, q, 0:80] + jnp.where(lane80 >= 64, halves[q], halves[q - 1])
                if par == 0:
                    value = jnp.where(sub80 == 0, 0.0, value)
                total.append(roll(value, 113))
            acc[par, 0] = jnp.where(lane80 >= 113, total[0], 0.0)
            for p in range(TILES):
                acc[par, p + 1] = jnp.where(lane80 < 113, total[p], total[p + 1])
            last = jnp.where(lane80 < 15, total[TILES], 0.0)
            acc[par, TILES + 1] = last
            acc[par, TILES + 1, 8:72] = last[8:72] + jnp.where(lane64 == 0, roll(q2_v[par, TILES - 1], 1), 0.0)

        for p in range(TILES):
            edge = jnp.concatenate([q1_v[1, p, PAIRS - 1 : PAIRS], jnp.zeros((7, 128), F32)], axis=0)
            acc[0, p + 1, 72:80] = acc[0, p + 1, 72:80] + edge
        for d, first in ((0, 0), (1, 72)):
            for par in (0, 1):
                for p in range(TILES):
                    row_out[fold, d, par, p] = acc[par, p + 1, first : first + 8]
        for s, (q, first_lane) in enumerate(((0, 112), (TILES + 1, 0))):
            col_out[fold, s] = packed(
                [acc[par, q, 8 + 16 * k : 24 + 16 * k] for par in (0, 1) for k in range(4)], first_lane, 16
            )
            for d, first in ((0, 0), (1, 72)):
                cor_out[fold, 2 * d + s] = packed(
                    [acc[par, q, first : first + 8] for par in (0, 1)], first_lane, 8
                )
        for copy in copies(fold):
            copy.start()

        for p in range(TILES):
            for par in (0, 1):
                m1, m2 = q1_v[par, p], q2_v[par, p]
                if par == 0:
                    above = jnp.concatenate([jnp.zeros((1, 128), F32), q1_v[1, p, : PAIRS - 1]], axis=0)
                else:
                    above = q1_v[0, p]
                    m1 = jnp.where((sub64 == PAIRS - 1) & bottom, 0.0, m1)
                before = roll(m2, 1)
                outer = roll(q2_v[par, p - 1], 1) if p else 0.0
                before = jnp.where(lane64 == 0, outer, before)
                if p + 1 == TILES:
                    m2 = jnp.where((lane64 == 127) & right, 0.0, m2)
                acc[par, p + 1, 8:72] = acc[par, p + 1, 8:72] - ((m1 - above) + (m2 - before))

        wait_in(fold)
        cols_add = [jnp.where(outside[2 + s], 0.0, col_in[fold, s]) for s in (0, 1)]
        cors_add = [jnp.where(outside[4 + s], 0.0, cor_in[fold, s]) for s in range(4)]
        for par in (0, 1):
            adds = []
            for s, first_lane in ((0, 0), (1, 112)):
                body = jnp.concatenate(
                    [unpacked(cols_add[s], 4 * par + k, first_lane) for k in range(4)], axis=0
                )
                zeros = jnp.zeros((PAIRS - 16, 128), F32)
                body = body + jnp.concatenate(
                    [unpacked(cors_add[s], par, first_lane), zeros, unpacked(cors_add[2 + s], par, first_lane)],
                    axis=0,
                )
                keep = lane64 < 15 if s == 0 else lane64 >= 113
                adds.append(jnp.where(keep, body, 0.0))
            for p in range(TILES):
                above = jnp.where(outside[0], 0.0, row_in[fold, 0, par, p])
                below = jnp.where(outside[1], 0.0, row_in[fold, 1, par, p])
                zeros = jnp.zeros((PAIRS - 16, 128), F32)
                value = acc[par, p + 1, 8:72] + jnp.concatenate([above, zeros, below], axis=0)
                if p == 0:
                    value = value + adds[0]
                if p + 1 == TILES:
                    value = value + adds[1]
                old = x_v[par, p]
                new = old - TAU * value
                x_v[par, p] = new
                bar_v[par, p] = 2.0 * new - old
        if step + 1 < ITERS:
            send_image(halo + 2)

    for par in (0, 1):
        for p in range(TILES):
            rows_of = pl.ds(par, PAIRS, stride=2)
            out_v[0, p, rows_of, :] = x_v[par, p]
            out_v[1, p, rows_of, :] = y_v[par, p]
    stores = [
        pltpu.make_async_copy(out_v.at[i, p], dst.at[:, slices[p]], store_sem.at[TILES * i + p])
        for i, dst in enumerate((restored_hbm, dual_out_hbm))
        for p in range(TILES)
    ]
    for store in stores:
        store.start()
    for store in stores:
        store.wait()


def per_device(observed, psf_table, psf_index, start_image, blur_dual, tv_dual):
    shape = observed.shape
    exchanges = 2 * ITERS
    block = (2, TILES, PAIRS, 128)
    tiled = (TILES, 2 * PAIRS, 128)
    hbm = pl.BlockSpec(memory_space=pl.ANY)
    return pl.pallas_call(
        kernel,
        out_shape=(jax.ShapeDtypeStruct(shape, F32), jax.ShapeDtypeStruct(shape, F32)),
        in_specs=[pl.BlockSpec(memory_space=pltpu.SMEM)] + [hbm] * 5,
        out_specs=(hbm, hbm),
        scratch_shapes=[
            pltpu.VMEM(tiled, F32),
            pltpu.VMEM(psf_table.shape, BF16),
            pltpu.VMEM(tiled, F32),
            pltpu.VMEM(tiled, F32),
            pltpu.VMEM((2,) + tiled, F32),
            pltpu.VMEM((2,) + tiled, F32),
            pltpu.VMEM((136, 128), F32),
            pltpu.VMEM((128, 128), F32),
            pltpu.VMEM((TILES * 4096, 128), BF16),
            pltpu.VMEM(block, F32),
            pltpu.VMEM(block, F32),
            pltpu.VMEM(block, F32),
            pltpu.VMEM(block, F32),
            pltpu.VMEM(block, F32),
            pltpu.VMEM(block, F32),
            pltpu.VMEM((2, 2, TILES, 88, 128), F32),
            pltpu.VMEM((2, TILES, 96, 128), F32),
            pltpu.VMEM((2, 2, TILES, 88, 128), F32),
            pltpu.VMEM((2, TILES + 2, 80, 128), F32),
            pltpu.VMEM((exchanges, 2, 2, TILES, 8, 128), F32),
            pltpu.VMEM((exchanges, 2, 16, 128), F32),
            pltpu.VMEM((exchanges, 4, 8, 128), F32),
            pltpu.VMEM((exchanges, 2, 2, TILES, 8, 128), F32),
            pltpu.VMEM((exchanges, 2, 16, 128), F32),
            pltpu.VMEM((exchanges, 4, 8, 128), F32),
            pltpu.SemaphoreType.DMA((4 * TILES + 1,)),
            pltpu.SemaphoreType.DMA((2 * TILES,)),
            pltpu.SemaphoreType.DMA((exchanges, 8)),
            pltpu.SemaphoreType.DMA((exchanges, 8)),
        ],
        compiler_params=pltpu.CompilerParams(collective_id=0, has_side_effects=True),
    )(psf_index, observed, psf_table, start_image, blur_dual, tv_dual)


def solution(mesh):
    placed = (
        P("row", "col"),
        P(),
        P("row", "col"),
        P("row", "col"),
        P("row", "col"),
        P(None, "row", "col"),
    )
    return jax.shard_map(
        per_device,
        mesh=mesh,
        in_specs=placed,
        out_specs=(P("row", "col"), P("row", "col")),
        check_vma=False,
    )
```

time: 170 us -> 47.8 us (0.28)
  the two profiles are of different devices: /device:TPU:27 before, /device:TPU:0 now
where the time goes in v1:
time: 47.8 us; the launch traced here: 47.6 us
  Pallas kernels  42 us (88%)
  local copies, waits for them, and re-layouts  4.99 us (10%)
  between operations  0.65 us (1%)
    pallas_call x1, Pallas kernels, per_device(): pl.pallas_call(kernel, out_shape=(jax.ShapeDtypeStruct(shape, F32), jax.S...  42 us
    unnamed x5, local copies, waits for them, and re-layouts  4.99 us

profile of v1, /device:TPU:0, one launch (start us, length us, event | category | flops | bytes accessed | tf_op | source)
XLA Modules:
  0.0 47.6 jit_solution(758657350873790249)
XLA Ops:
  0.6 2.6 %copy.8.table_hbm = bf16[64,31,31]{2,1,0:T(8,128)(2,1)} copy(bf16[64,31,31]{0,2,1:T(8,128)(2,1)} %param.7) | data formatting | bytes 246016 | tf_op args[1]
  3.2 42.0 %shard_map.77 = (f32[128,512]{1,0:T(8,128)}, f32[128,512]{1,0:T(8,128)}) custom-call(s32[1,4]{1,0:T(1,128)} %index_ref.1, f32[128,512]{1,0:T(8,128)} %observed_hbm.1, bf16[64,31,31]{2,1,0:T(8,128)(2,1)} %copy.8.table_hbm, f32[128,512]{1,0:T(8,128)} %start_hbm.1, f32[128,512]{1,0:T(8,128)} %dual_hbm.1, f32[2,128,512]{2,1,0:T(8,128)} %tv_hbm.1), custom_call_target="tpu_custom_call" | custom-call | tf_op jit(solution)/shard_map/pallas_call | solution.py:381
  45.2 0.0 copy-start
  45.2 1.7 %copy.11 = f32[128,512]{1,0:T(8,128)} copy(f32[128,512]{1,0:T(8,128)} %get-tuple-element.4) | data formatting | bytes 524288
  46.9 0.0 copy-done
  46.9 0.7 %copy.12 = f32[128,512]{1,0:T(8,128)} copy(f32[128,512]{1,0:T(8,128)S(1)} %copy-done) | data formatting | bytes 524288
Async XLA Ops:
  45.2 1.7 %copy-start = (f32[128,512]{1,0:T(8,128)S(1)}, f32[128,512]{1,0:T(8,128)}, u32[]{:S(2)}) copy-start(f32[128,512]{1,0:T(8,128)} %get-tuple-element.5) | copy-start | bytes 786436

commit v2 on v1

--- a/solution.py
+++ b/solution.py
@@ -13,6 +13,7 @@
 PAIRS = 64
 TILES = 4
 DIRS = ((-1, 0), (1, 0), (0, -1), (0, 1), (-1, -1), (-1, 1), (1, -1), (1, 1))
+OPPOSITE = (1, 0, 3, 2, 7, 6, 5, 4)
 MESH_ID = pl.DeviceIdType.MESH
 F32 = jnp.float32
 BF16 = jnp.bfloat16
@@ -29,11 +30,11 @@
 
 def kernel(
     index_ref, observed_hbm, table_hbm, start_hbm, dual_hbm, tv_hbm,
-    restored_hbm, dual_out_hbm,
-    start_v, table_v, observed_v, dual_v, tv_v, out_v,
-    kern_v, base_v, weights, x_v, bar_v, obs_v, y_v, q1_v, q2_v, shifted, ypad, spread, acc,
+    restored_ref, dual_out_ref,
+    start_v, table_v, observed_v, dual_v, tv_v,
+    base_v, weights, x_v, bar_v, obs_v, y_v, q1_v, q2_v, shifted, ypad, spread, acc,
     row_out, col_out, cor_out, row_in, col_in, cor_in,
-    load_sem, store_sem, send_sem, recv_sem,
+    load_sem, send_sem, recv_sem,
 ):
     row, col = lax.axis_index("row"), lax.axis_index("col")
     rows, cols = lax.axis_size("row"), lax.axis_size("col")
@@ -42,9 +43,16 @@
         dr, dc = direction
         return (lax.rem(row + dr + rows, rows), lax.rem(col + dc + cols, cols))
 
+    top, bottom = row == 0, row == rows - 1
+    left, right = col == 0, col == cols - 1
+    outside = (top, bottom, left, right, top | left, top | right, bottom | left, bottom | right)
+    inside = [jnp.logical_not(o) for o in outside]
+
     barrier = pltpu.get_barrier_semaphore()
-    for direction in DIRS:
-        pl.semaphore_signal(barrier, inc=1, device_id=at(direction), device_id_type=MESH_ID)
+    for d, direction in enumerate(DIRS):
+        @pl.when(inside[d])
+        def _():
+            pl.semaphore_signal(barrier, inc=1, device_id=at(direction), device_id_type=MESH_ID)
 
     slices = [slice(128 * p, 128 * p + 128) for p in range(TILES)]
     plain = ((start_hbm, start_v), (observed_hbm, observed_v), (dual_hbm, dual_v))
@@ -55,9 +63,6 @@
     for load in loads:
         load.start()
 
-    top, bottom = row == 0, row == rows - 1
-    left, right = col == 0, col == cols - 1
-    outside = (top, bottom, left, right, top | left, top | right, bottom | left, bottom | right)
     lane64 = lanes((PAIRS, 128))
     lane8 = lanes((8, 128))
     lane16 = lanes((16, 128))
@@ -72,7 +77,7 @@
                 src, dst = col_out.at[exchange, d - 2], col_in.at[exchange, (d - 2) ^ 1]
             else:
                 src, dst = cor_out.at[exchange, d - 4], cor_in.at[exchange, 3 - (d - 4)]
-            back = d ^ 1 if d < 4 else 4 + 3 - (d - 4)
+            back = OPPOSITE[d]
             result.append(
                 pltpu.make_async_remote_copy(
                     src_ref=src,
@@ -85,9 +90,17 @@
             )
         return result
 
+    def start_out(exchange):
+        for d, copy in enumerate(copies(exchange)):
+            pl.when(inside[d])(copy.start)
+
     def wait_in(exchange):
-        for copy in copies(exchange):
-            copy.wait()
+        for d, copy in enumerate(copies(exchange)):
+            pl.when(inside[OPPOSITE[d]])(copy.wait_recv)
+
+    def wait_out(exchange):
+        for d, copy in enumerate(copies(exchange)):
+            pl.when(inside[d])(copy.wait_send)
 
     def packed(parts, first_lane, height):
         lane = lane16 if height == 16 else lane8
@@ -121,38 +134,64 @@
                 cor_out[exchange, 2 * d + s] = packed(
                     [bar_v[par, p, first : first + 8] for par in (0, 1)], first_lane, 8
                 )
-        for copy in copies(exchange):
-            copy.start()
-
-    pl.semaphore_wait(barrier, len(DIRS))
+        start_out(exchange)
+
+    pl.semaphore_wait(barrier, sum(i.astype(jnp.int32) for i in inside))
     send_image(0)
 
-    kern_v[...] = jnp.zeros_like(kern_v)
     loads[TILES].wait()
+    which = lax.broadcasted_iota(jnp.int32, (8, 64), 0) & 3
+    entry = lanes((8, 64))
+    chosen = jnp.zeros((8, 64), F32)
     for p in range(TILES):
-        table = table_v[index_ref[0, p]].astype(F32)
-        kern_v[8 + 32 * p : 8 + 32 * p + TAPS, 0:TAPS] = table / jnp.sum(table)
+        chosen = jnp.where((which == p) & (entry == index_ref[0, p]), 1.0, chosen)
+    chosen = chosen.astype(BF16)
+    gap = jnp.zeros((1, 64), F32)
+    lines = [
+        jnp.concatenate([table_v[a].astype(F32), gap], axis=0).astype(BF16)
+        if a < TAPS else jnp.zeros((32, 64), BF16)
+        for a in range(32)
+    ]
+    picked = jnp.concatenate(
+        [
+            lax.dot_general(
+                chosen,
+                jnp.concatenate(lines[8 * k : 8 * k + 8], axis=0),
+                (((1,), (1,)), ((), ())),
+                preferred_element_type=F32,
+            )
+            for k in range(4)
+        ],
+        axis=1,
+    )
+    normed = picked / jnp.sum(picked, axis=1, keepdims=True)
+    kernels = jnp.concatenate([normed[:, 128 * q : 128 * q + 128] for q in range(8)], axis=0)
+    before = jnp.concatenate([jnp.zeros((8, 128), F32), kernels[:56]], axis=0)
+    kernels, before = kernels.astype(BF16), before.astype(BF16)
     tap = lax.broadcasted_iota(jnp.int32, (128, 128), 0)
     place = lanes((128, 128))
-    flip_low = ((tap < TAPS) & (place == lax.rem(128 - tap, 128))).astype(F32).astype(BF16)
-    flip_high = ((tap < TAPS) & (place == 64 - tap)).astype(F32).astype(BF16)
-    base_v[...] = jnp.dot(kern_v[8:136].astype(BF16), flip_low, preferred_element_type=F32) + jnp.dot(
-        kern_v[7:135].astype(BF16), flip_high, preferred_element_type=F32
-    )
+
+    def flip(r, first):
+        hit = ((tap >> 5) == r) & (place == ((first - (tap & 31)) & 127))
+        return hit.astype(F32).astype(BF16)
+
+    for r in range(4):
+        low = jnp.dot(kernels, flip(r, 128), preferred_element_type=F32)
+        high = jnp.dot(kernels if r else before, flip((r - 1) & 3, 64), preferred_element_type=F32)
+        base_v[r] = low + high
     reach = tap - (place & 63)
     band = (reach >= 0) & (reach < TAPS)
 
-    unroll = 4
-
     def build(step, carry):
-        for u in range(unroll):
-            r = step * unroll + u
-            line = jnp.broadcast_to(base_v[pl.ds(r, 1), :], (128, 128))
+        q, p = step >> 2, step & 3
+        for r in range(4):
+            line = jnp.broadcast_to(base_v[r, pl.ds(q * 8 + p, 1), :], (128, 128))
             rolled = pltpu.roll(line, 0, 1, stride=1, stride_axis=0)
-            weights[pl.ds(pl.multiple_of(r * 128, 128), 128), :] = jnp.where(band, rolled, 0.0).astype(BF16)
+            start = pl.multiple_of(p * 4096 + (q * 4 + r) * 128, 128)
+            weights[pl.ds(start, 128), :] = jnp.where(band, rolled, 0.0).astype(BF16)
         return carry
 
-    lax.fori_loop(0, 128 // unroll, build, 0)
+    lax.fori_loop(0, 32, build, 0)
 
     ypad[...] = jnp.zeros_like(ypad)
     for load in loads[TILES + 1 :]:
@@ -306,8 +345,7 @@
                 cor_out[fold, 2 * d + s] = packed(
                     [acc[par, q, first : first + 8] for par in (0, 1)], first_lane, 8
                 )
-        for copy in copies(fold):
-            copy.start()
+        start_out(fold)
 
         for p in range(TILES):
             for par in (0, 1):
@@ -359,11 +397,16 @@
     for par in (0, 1):
         for p in range(TILES):
             rows_of = pl.ds(par, PAIRS, stride=2)
-            out_v[0, p, rows_of, :] = x_v[par, p]
-            out_v[1, p, rows_of, :] = y_v[par, p]
+            restored_ref[p, rows_of, :] = x_v[par, p]
+            dual_out_ref[p, rows_of, :] = y_v[par, p]
+    for exchange in range(2 * ITERS):
+        wait_out(exchange)
+
+
+def put_out(restored_ref, dual_ref, restored_hbm, dual_hbm, store_sem):
     stores = [
-        pltpu.make_async_copy(out_v.at[i, p], dst.at[:, slices[p]], store_sem.at[TILES * i + p])
-        for i, dst in enumerate((restored_hbm, dual_out_hbm))
+        pltpu.make_async_copy(src.at[p], dst.at[:, 128 * p : 128 * p + 128], store_sem.at[TILES * i + p])
+        for i, (src, dst) in enumerate(((restored_ref, restored_hbm), (dual_ref, dual_hbm)))
         for p in range(TILES)
     ]
     for store in stores:
@@ -378,20 +421,19 @@
     block = (2, TILES, PAIRS, 128)
     tiled = (TILES, 2 * PAIRS, 128)
     hbm = pl.BlockSpec(memory_space=pl.ANY)
-    return pl.pallas_call(
+    table = psf_table.transpose(1, 2, 0)
+    results = pl.pallas_call(
         kernel,
-        out_shape=(jax.ShapeDtypeStruct(shape, F32), jax.ShapeDtypeStruct(shape, F32)),
+        out_shape=(pltpu.VMEM(tiled, F32), pltpu.VMEM(tiled, F32)),
         in_specs=[pl.BlockSpec(memory_space=pltpu.SMEM)] + [hbm] * 5,
-        out_specs=(hbm, hbm),
+        out_specs=(pl.BlockSpec(memory_space=pltpu.VMEM),) * 2,
         scratch_shapes=[
             pltpu.VMEM(tiled, F32),
-            pltpu.VMEM(psf_table.shape, BF16),
+            pltpu.VMEM(table.shape, BF16),
             pltpu.VMEM(tiled, F32),
             pltpu.VMEM(tiled, F32),
             pltpu.VMEM((2,) + tiled, F32),
-            pltpu.VMEM((2,) + tiled, F32),
-            pltpu.VMEM((136, 128), F32),
-            pltpu.VMEM((128, 128), F32),
+            pltpu.VMEM((4, 64, 128), F32),
             pltpu.VMEM((TILES * 4096, 128), BF16),
             pltpu.VMEM(block, F32),
             pltpu.VMEM(block, F32),
@@ -410,12 +452,18 @@
             pltpu.VMEM((exchanges, 2, 16, 128), F32),
             pltpu.VMEM((exchanges, 4, 8, 128), F32),
             pltpu.SemaphoreType.DMA((4 * TILES + 1,)),
-            pltpu.SemaphoreType.DMA((2 * TILES,)),
             pltpu.SemaphoreType.DMA((exchanges, 8)),
             pltpu.SemaphoreType.DMA((exchanges, 8)),
         ],
         compiler_params=pltpu.CompilerParams(collective_id=0, has_side_effects=True),
-    )(psf_index, observed, psf_table, start_image, blur_dual, tv_dual)
+    )(psf_index, observed, table, start_image, blur_dual, tv_dual)
+    return pl.pallas_call(
+        put_out,
+        out_shape=(jax.ShapeDtypeStruct(shape, F32), jax.ShapeDtypeStruct(shape, F32)),
+        in_specs=[hbm] * 2,
+        out_specs=(hbm, hbm),
+        scratch_shapes=[pltpu.SemaphoreType.DMA((2 * TILES,))],
+    )(*(pltpu.with_memory_space_constraint(result, pltpu.VMEM) for result in results))
 
 
 def solution(mesh):

time: 47.8 us -> 36.8 us (0.77)
  the two profiles are of different devices: /device:TPU:0 before, /device:TPU:27 now
where the time goes in v2:
time: 36.8 us; the launch traced here: 36.7 us
  Pallas kernels  36 us (98%)
  between operations  0.64 us (2%)
    pallas_call x1, Pallas kernels, per_device(): pl.pallas_call(kernel, out_shape=(pltpu.VMEM(tiled, F32), pltpu.VMEM(tile...  35.2 us
    pallas_call x1, Pallas kernels, per_device(): pl.pallas_call(put_out, out_shape=(jax.ShapeDtypeStruct(shape, F32), jax....  0.85 us

profile of v2, /device:TPU:27, one launch (start us, length us, event | category | flops | bytes accessed | tf_op | source)
XLA Modules:
  0.0 36.7 jit_solution(987307474967758309)
XLA Ops:
  0.6 35.2 %shard_map.77 = (f32[4,128,128]{2,1,0:T(8,128)S(1)}, f32[4,128,128]{2,1,0:T(8,128)S(1)}) custom-call(s32[1,4]{1,0:T(1,128)} %index_ref.1, f32[128,512]{1,0:T(8,128)} %observed_hbm.1, bf16[31,31,64]{2,1,0:T(8,128)(2,1)} %bitcast.1, f32[128,512]{1,0:T(8,128)} %start_hbm.1, f32[128,512]{1,0:T(8,128)} %dual_hbm.1, f32[2,128,512]{2,1,0:T(8,128)} %tv_hbm.1), custom_call_target="tpu_custom_call" | custom-call | tf_op jit(solution)/shard_map/pallas_call | solution.py:425
  35.8 0.9 %shard_map.78 = (f32[128,512]{1,0:T(8,128)}, f32[128,512]{1,0:T(8,128)}) custom-call(f32[4,128,128]{2,1,0:T(8,128)S(1)} %get-tuple-element.4.restored_ref, f32[4,128,128]{2,1,0:T(8,128)S(1)} %get-tuple-element.5.dual_ref), custom_call_target="tpu_custom_call" | custom-call | tf_op jit(solution)/shard_map/pallas_call | solution.py:460

commit v3 on v2

--- a/solution.py
+++ b/solution.py
@@ -28,11 +28,14 @@
     return value if shift == 0 else pltpu.roll(value, shift, 1)
 
 
+T_ROWS = 17 * 128
+
+
 def kernel(
     index_ref, observed_hbm, table_hbm, start_hbm, dual_hbm, tv_hbm,
     restored_ref, dual_out_ref,
     start_v, table_v, observed_v, dual_v, tv_v,
-    base_v, weights, x_v, bar_v, obs_v, y_v, q1_v, q2_v, shifted, ypad, spread, acc,
+    base_v, weights, weights_t, x_v, bar_v, obs_v, y_v, q1_v, q2_v, shifted, shifted_halo, blur_v, ypad, spread,
     row_out, col_out, cor_out, row_in, col_in, cor_in,
     load_sem, send_sem, recv_sem,
 ):
@@ -175,25 +178,40 @@
         hit = ((tap >> 5) == r) & (place == ((first - (tap & 31)) & 127))
         return hit.astype(F32).astype(BF16)
 
+    lane_of = lanes((64, 128))
     for r in range(4):
         low = jnp.dot(kernels, flip(r, 128), preferred_element_type=F32)
         high = jnp.dot(kernels if r else before, flip((r - 1) & 3, 64), preferred_element_type=F32)
         base_v[r] = low + high
+        base_v[4 + r] = jnp.where(lane_of < 32, roll(kernels.astype(F32), -32 * r), 0.0)
     reach = tap - (place & 63)
     band = (reach >= 0) & (reach < TAPS)
-
-    def build(step, carry):
-        q, p = step >> 2, step & 3
-        for r in range(4):
-            line = jnp.broadcast_to(base_v[r, pl.ds(q * 8 + p, 1), :], (128, 128))
-            rolled = pltpu.roll(line, 0, 1, stride=1, stride_axis=0)
-            start = pl.multiple_of(p * 4096 + (q * 4 + r) * 128, 128)
-            weights[pl.ds(start, 128), :] = jnp.where(band, rolled, 0.0).astype(BF16)
+    for p in range(TILES):
+        weights_t[p * T_ROWS + 64 : p * T_ROWS + 128, 0:128] = jnp.zeros((64, 128), BF16)
+
+    def build(q, carry):
+        for p in range(TILES):
+            for r in range(4):
+                line = base_v[r, pl.ds(q * 8 + p, 1), :]
+                rolled = pltpu.roll(jnp.broadcast_to(line, (128, 128)), 0, 1, stride=1, stride_axis=0)
+                start = pl.multiple_of(p * 4096 + (q * 4 + r) * 128, 128)
+                weights[pl.ds(start, 128), :] = jnp.where(band, rolled, 0.0).astype(BF16)
+                line = base_v[4 + r, pl.ds(q * 8 + p, 1), :]
+                rolled = pltpu.roll(jnp.broadcast_to(line, (64, 128)), 0, 1, stride=1, stride_axis=0).astype(BF16)
+                for d in (0, 1):
+                    t, e = (r + d) >> 1, (r + d) & 1
+                    start = pl.multiple_of(p * T_ROWS + (q * 2 + t) * 128 + d * 64, 64)
+                    weights_t[pl.ds(start, 64), 128 * e : 128 * e + 128] = rolled
         return carry
 
-    lax.fori_loop(0, 32, build, 0)
+    lax.fori_loop(0, 8, build, 0)
 
     ypad[...] = jnp.zeros_like(ypad)
+    shifted[...] = jnp.zeros_like(shifted)
+    shifted_halo[...] = jnp.zeros_like(shifted_halo)
+    for h in (0, 1):
+        for p in range(TILES):
+            spread[0, h, p, 0:8] = jnp.zeros((8, 128), F32)
     for load in loads[TILES + 1 :]:
         load.wait()
     for par in (0, 1):
@@ -204,8 +222,75 @@
             q1_v[par, p] = tv_v[0, p, rows_of, :]
             q2_v[par, p] = tv_v[1, p, rows_of, :]
 
+    def stacked_rows(source, p, ranges):
+        pieces = []
+        for t in range(16):
+            for par in (1, 0):
+                first = t + 1 - par
+                pieces.append(
+                    jnp.concatenate(
+                        [source[par, h, p, a + first : a + first + n] for h, a, n in ranges], axis=0
+                    ).astype(BF16)
+                )
+        return jnp.concatenate(pieces, axis=1)
+
+    def lay(target, tiles, par, first, count):
+        lane = lanes((count, 128))
+        by15 = [0.0 if t is None else roll(t, 15) for t in tiles[:-1]]
+        by79 = [0.0 if t is None else roll(t, 79) for t in tiles[1:]]
+        for p in range(TILES):
+            target[par, 0, p, first : first + count] = jnp.where(lane < 15, by15[p], by15[p + 1])
+            target[par, 1, p, first : first + count] = jnp.where(lane < 79, by79[p], by79[p + 1])
+
+    def blur_own(p, carry):
+        lhs = stacked_rows(shifted, p, ((0, 0, PAIRS), (1, 0, PAIRS)))
+        matrix = weights[pl.ds(pl.multiple_of(p * 4096, 4096), 4096), :]
+        blur_v[p] = jnp.dot(lhs, matrix, preferred_element_type=F32)
+        return carry
+
+    def tv(par, p, a, b, below, beyond):
+        value = bar_v[par, p, a:b]
+        if par == 0:
+            grad1 = bar_v[1, p, a:b] - value
+        elif b < PAIRS:
+            grad1 = bar_v[0, p, a + 1 : b + 1] - value
+        else:
+            grad1 = jnp.concatenate([bar_v[0, p, a + 1 : b], below], axis=0) - value
+            grad1 = jnp.where((lax.broadcasted_iota(jnp.int32, (b - a, 128), 0) == b - a - 1) & bottom, 0.0, grad1)
+        if p + 1 < TILES:
+            beyond = bar_v[par, p + 1, a:b]
+        lane = lanes((b - a, 128))
+        grad2 = jnp.where(lane < 127, roll(value, 127), roll(beyond, 127)) - value
+        if p + 1 == TILES:
+            grad2 = jnp.where((lane == 127) & right, 0.0, grad2)
+        u1 = q1_v[par, p, a:b] + SIGMA * grad1
+        u2 = q2_v[par, p, a:b] + SIGMA * grad2
+        shrink = jnp.maximum(1.0, jnp.sqrt(u1 * u1 + u2 * u2) / WEIGHT)
+        q1_v[par, p, a:b] = u1 / shrink
+        q2_v[par, p, a:b] = u2 / shrink
+
+    def merged(par, q, a, b):
+        lane = lanes((b - a, 128))
+        if q == 0:
+            value = spread[par, 0, 0, a:b] + jnp.where(lane >= 64, roll(spread[par, 1, 0, a:b], 64), 0.0)
+        elif q == TILES:
+            value = jnp.where(lane < 64, roll(spread[par, 1, q - 1, a:b], 64), 0.0)
+        else:
+            value = spread[par, 0, q, a:b] + jnp.where(
+                lane >= 64, roll(spread[par, 1, q, a:b], 64), roll(spread[par, 1, q - 1, a:b], 64)
+            )
+        return roll(value, 113)
+
     for step in range(ITERS):
         halo, fold = 2 * step, 2 * step + 1
+
+        for par in (0, 1):
+            lay(shifted, [None] + [bar_v[par, p] for p in range(TILES)] + [None], par, 8, PAIRS)
+        lax.fori_loop(0, TILES, blur_own, 0)
+        for p in range(TILES - 1):
+            tv(0, p, 0, PAIRS, None, None)
+            tv(1, p, 0, PAIRS - 8, None, None)
+
         wait_in(halo)
         rows_in = [
             [
@@ -216,30 +301,11 @@
         ]
         cols_in = [jnp.where(outside[2 + s], 0.0, col_in[halo, s]) for s in (0, 1)]
         cors_in = [jnp.where(outside[4 + s], 0.0, cor_in[halo, s]) for s in range(4)]
-
-        def sides(par, first_lanes):
-            return [
-                jnp.concatenate(
-                    [unpacked(cols_in[s], 4 * par + k, first_lanes[s]) for k in range(4)], axis=0
-                )
-                for s in (0, 1)
-            ]
-
-        def lay(tiles, par, first, count):
-            lane = lanes((count, 128))
-            by15 = [roll(t, 15) for t in tiles[:-1]]
-            by79 = [roll(t, 79) for t in tiles[1:]]
-            for p in range(TILES):
-                shifted[par, 0, p, first : first + count] = jnp.where(lane < 15, by15[p], by15[p + 1])
-                shifted[par, 1, p, first : first + count] = jnp.where(lane < 79, by79[p], by79[p + 1])
-
-        side_tiles = [sides(par, (112, 0)) for par in (0, 1)]
-        for par in (0, 1):
-            lay(
-                [side_tiles[par][0]] + [bar_v[par, p] for p in range(TILES)] + [side_tiles[par][1]], par, 8, PAIRS
-            )
+        beyond = []
+        for par in (0, 1):
             for d, first in ((0, 0), (1, 72)):
                 lay(
+                    shifted_halo,
                     [unpacked(cors_in[2 * d], par, 112)]
                     + rows_in[d][par]
                     + [unpacked(cors_in[2 * d + 1], par, 0)],
@@ -247,22 +313,45 @@
                     first,
                     8,
                 )
-
-        def blur(p, carry):
-            pieces = []
-            for t in range(16):
-                pieces.append(
-                    jnp.concatenate([shifted[0 + 1, h, p, t : t + PAIRS] for h in (0, 1)], axis=0).astype(BF16)
-                )
-                pieces.append(
-                    jnp.concatenate([shifted[0, h, p, t + 1 : t + 1 + PAIRS] for h in (0, 1)], axis=0).astype(BF16)
-                )
-            stacked = jnp.concatenate(pieces, axis=1)
-            matrix = weights[pl.ds(pl.multiple_of(p * 4096, 4096), 4096), :]
-            blurred = jnp.dot(stacked, matrix, preferred_element_type=F32)
-            first, second = blurred[:PAIRS], blurred[PAIRS:]
-            even = jnp.where(lane64 < 64, first, roll(second, 64))
-            odd = jnp.where(lane64 < 64, roll(first, 64), second)
+            for k in range(4):
+                side = [unpacked(cols_in[0], 4 * par + k, 112 + 15), unpacked(cols_in[1], 4 * par + k, 79)]
+                place_k = slice(8 + 16 * k, 24 + 16 * k)
+                shifted_halo[par, 0, 0, place_k] = jnp.where(lane16 < 15, side[0], 0.0)
+                shifted_halo[par, 1, TILES - 1, place_k] = jnp.where(lane16 < 79, 0.0, side[1])
+            beyond.append(jnp.concatenate([unpacked(cols_in[1], 4 * par + k, 0) for k in range(4)], axis=0))
+
+        gap48 = jnp.zeros((PAIRS - 16, 128), F32)
+
+        def rows_full(p):
+            return 0 if p == 0 else 1 if p + 1 == TILES else None
+
+        def blur_halo(p):
+            full = rows_full(p)
+            ranges = [(full, 0, PAIRS)] if full is not None else []
+            for h in (0, 1):
+                if h != full:
+                    ranges += [(h, 0, 8), (h, PAIRS - 8, 8)]
+            return jnp.dot(
+                stacked_rows(shifted_halo, p, ranges),
+                weights[p * 4096 : p * 4096 + 4096],
+                preferred_element_type=F32,
+            )
+
+        def dual(p, extra):
+            full = rows_full(p)
+            halves, place_r = [None, None], 0
+            if full is not None:
+                halves[full] = blur_v[p, PAIRS * full : PAIRS * full + PAIRS] + extra[:PAIRS]
+                place_r = PAIRS
+            for h in (0, 1):
+                if h != full:
+                    more = jnp.concatenate(
+                        [extra[place_r : place_r + 8], gap48, extra[place_r + 8 : place_r + 16]], axis=0
+                    )
+                    halves[h] = blur_v[p, PAIRS * h : PAIRS * h + PAIRS] + more
+                    place_r += 16
+            even = jnp.where(lane64 < 64, halves[0], roll(halves[1], 64))
+            odd = jnp.where(lane64 < 64, roll(halves[0], 64), halves[1])
             new = []
             for par, value in ((0, even), (1, odd)):
                 updated = (y_v[par, p] + SIGMA * (value - obs_v[par, p])) / (1.0 + SIGMA)
@@ -270,135 +359,113 @@
                 new.append(updated)
             ypad[0, p, 16 : 16 + PAIRS] = jnp.where(lane64 < 64, new[0], roll(new[1], 64))
             ypad[1, p, 16 : 16 + PAIRS] = jnp.where(lane64 < 64, roll(new[0], 64), new[1])
-            return carry
-
-        lax.fori_loop(0, TILES, blur, 0)
-
-        for p in range(TILES):
-            even, odd = bar_v[0, p], bar_v[1, p]
-            below = jnp.concatenate([even[1:], rows_in[1][0][p][:1]], axis=0)
-            grad_even = odd - even
-            grad_odd = jnp.where((sub64 == PAIRS - 1) & bottom, 0.0, below - odd)
-            for par, value, grad1 in ((0, even, grad_even), (1, odd, grad_odd)):
-                beyond = bar_v[par, p + 1] if p + 1 < TILES else side_tiles[par][1]
-                after = jnp.where(lane64 < 127, roll(value, 127), roll(beyond, 127))
-                grad2 = after - value
-                if p + 1 == TILES:
-                    grad2 = jnp.where((lane64 == 127) & right, 0.0, grad2)
-                u1 = q1_v[par, p] + SIGMA * grad1
-                u2 = q2_v[par, p] + SIGMA * grad2
-                shrink = jnp.maximum(1.0, jnp.sqrt(u1 * u1 + u2 * u2) / WEIGHT)
-                q1_v[par, p] = u1 / shrink
-                q2_v[par, p] = u2 / shrink
-
-        def adjoint(p, carry):
-            pieces = [
-                jnp.concatenate([ypad[h, p, 16 - t : 96 - t] for h in (0, 1)], axis=0).astype(BF16)
-                for t in range(16)
-            ]
-            stacked = jnp.concatenate(pieces, axis=1)
-            start = pl.multiple_of(p * 4096, 4096)
-            matrix = jnp.concatenate(
-                [weights[pl.ds(start + 256 * t, 256), :] for t in range(16)], axis=1
-            )
-            out = lax.dot_general(stacked, matrix, (((1,), (1,)), ((), ())), preferred_element_type=F32)
+
+        def adjoint(p):
+            out = jnp.dot(
+                jnp.concatenate(
+                    [
+                        jnp.concatenate([ypad[h, p, 16 - t : 96 - t] for h in (0, 1)], axis=0).astype(BF16)
+                        for t in range(16)
+                    ],
+                    axis=1,
+                ),
+                weights_t[p * T_ROWS : p * T_ROWS + 2048],
+                preferred_element_type=F32,
+            )
             for h in (0, 1):
                 spread[1, h, p, 0:80] = out[80 * h : 80 * h + 80, 0:128]
                 spread[0, h, p, 1:81] = out[80 * h : 80 * h + 80, 128:256]
-            return carry
-
-        lax.fori_loop(0, TILES, adjoint, 0)
-        lane80 = lanes((80, 128))
-        sub80 = lax.broadcasted_iota(jnp.int32, (80, 128), 0)
-        for par in (0, 1):
-            halves = [roll(spread[par, 1, p, 0:80], 64) for p in range(TILES)]
-            total = []
-            for q in range(TILES + 1):
-                if q == 0:
-                    value = spread[par, 0, 0, 0:80] + jnp.where(lane80 >= 64, halves[0], 0.0)
-                elif q == TILES:
-                    value = jnp.where(lane80 < 64, halves[q - 1], 0.0)
-                else:
-                    value = spread[par, 0, q, 0:80] + jnp.where(lane80 >= 64, halves[q], halves[q - 1])
-                if par == 0:
-                    value = jnp.where(sub80 == 0, 0.0, value)
-                total.append(roll(value, 113))
-            acc[par, 0] = jnp.where(lane80 >= 113, total[0], 0.0)
+
+        extras = [blur_halo(p) for p in range(TILES)]
+        for p in range(TILES):
+            dual(p, extras[p])
+        for p in range(TILES):
+            adjoint(p)
+
+        for p in range(TILES - 1):
+            tv(1, p, PAIRS - 8, PAIRS, rows_in[1][0][p][:1], None)
+        for par in (0, 1):
+            tv(par, TILES - 1, 0, PAIRS, rows_in[1][0][TILES - 1][:1], beyond[par])
+
+        corners = [[None, None] for _ in range(4)]
+        for par in (0, 1):
+            for d, (a, b) in ((0, (0, 8)), (1, (72, 80))):
+                tiles = [merged(par, q, a, b) for q in range(TILES + 1)]
+                for p in range(TILES):
+                    value = jnp.where(lane8 < 113, tiles[p], tiles[p + 1])
+                    if d == 1 and par == 0:
+                        value = value + jnp.concatenate(
+                            [q1_v[1, p, PAIRS - 1 : PAIRS], jnp.zeros((7, 128), F32)], axis=0
+                        )
+                    row_out[fold, d, par, p] = value
+                corners[2 * d][par] = jnp.where(lane8 >= 113, tiles[0], 0.0)
+                corners[2 * d + 1][par] = jnp.where(lane8 < 15, tiles[TILES], 0.0)
+        sides = [[None, None], [None, None]]
+        for par in (0, 1):
+            sides[0][par] = jnp.where(lane64 >= 113, merged(par, 0, 8, 72), 0.0)
+            sides[1][par] = jnp.where(lane64 < 15, merged(par, TILES, 8, 72), 0.0) + jnp.where(
+                lane64 == 0, roll(q2_v[par, TILES - 1], 1), 0.0
+            )
+        for s, first_lane in enumerate((112, 0)):
+            col_out[fold, s] = packed(
+                [sides[s][par][16 * k : 16 * k + 16] for par in (0, 1) for k in range(4)], first_lane, 16
+            )
+            for d in (0, 1):
+                cor_out[fold, 2 * d + s] = packed(corners[2 * d + s], first_lane, 8)
+        start_out(fold)
+
+        for par in (0, 1):
+            tiles = [merged(par, q, 8, 72) for q in range(TILES + 1)]
             for p in range(TILES):
-                acc[par, p + 1] = jnp.where(lane80 < 113, total[p], total[p + 1])
-            last = jnp.where(lane80 < 15, total[TILES], 0.0)
-            acc[par, TILES + 1] = last
-            acc[par, TILES + 1, 8:72] = last[8:72] + jnp.where(lane64 == 0, roll(q2_v[par, TILES - 1], 1), 0.0)
-
-        for p in range(TILES):
-            edge = jnp.concatenate([q1_v[1, p, PAIRS - 1 : PAIRS], jnp.zeros((7, 128), F32)], axis=0)
-            acc[0, p + 1, 72:80] = acc[0, p + 1, 72:80] + edge
-        for d, first in ((0, 0), (1, 72)):
-            for par in (0, 1):
-                for p in range(TILES):
-                    row_out[fold, d, par, p] = acc[par, p + 1, first : first + 8]
-        for s, (q, first_lane) in enumerate(((0, 112), (TILES + 1, 0))):
-            col_out[fold, s] = packed(
-                [acc[par, q, 8 + 16 * k : 24 + 16 * k] for par in (0, 1) for k in range(4)], first_lane, 16
-            )
-            for d, first in ((0, 0), (1, 72)):
-                cor_out[fold, 2 * d + s] = packed(
-                    [acc[par, q, first : first + 8] for par in (0, 1)], first_lane, 8
-                )
-        start_out(fold)
-
-        for p in range(TILES):
-            for par in (0, 1):
+                value = jnp.where(lane64 < 113, tiles[p], tiles[p + 1])
                 m1, m2 = q1_v[par, p], q2_v[par, p]
                 if par == 0:
                     above = jnp.concatenate([jnp.zeros((1, 128), F32), q1_v[1, p, : PAIRS - 1]], axis=0)
                 else:
                     above = q1_v[0, p]
                     m1 = jnp.where((sub64 == PAIRS - 1) & bottom, 0.0, m1)
-                before = roll(m2, 1)
                 outer = roll(q2_v[par, p - 1], 1) if p else 0.0
-                before = jnp.where(lane64 == 0, outer, before)
+                before = jnp.where(lane64 == 0, outer, roll(m2, 1))
                 if p + 1 == TILES:
                     m2 = jnp.where((lane64 == 127) & right, 0.0, m2)
-                acc[par, p + 1, 8:72] = acc[par, p + 1, 8:72] - ((m1 - above) + (m2 - before))
-
-        wait_in(fold)
-        cols_add = [jnp.where(outside[2 + s], 0.0, col_in[fold, s]) for s in (0, 1)]
-        cors_add = [jnp.where(outside[4 + s], 0.0, cor_in[fold, s]) for s in range(4)]
-        for par in (0, 1):
-            adds = []
-            for s, first_lane in ((0, 0), (1, 112)):
-                body = jnp.concatenate(
-                    [unpacked(cols_add[s], 4 * par + k, first_lane) for k in range(4)], axis=0
-                )
-                zeros = jnp.zeros((PAIRS - 16, 128), F32)
-                body = body + jnp.concatenate(
-                    [unpacked(cors_add[s], par, first_lane), zeros, unpacked(cors_add[2 + s], par, first_lane)],
-                    axis=0,
-                )
-                keep = lane64 < 15 if s == 0 else lane64 >= 113
-                adds.append(jnp.where(keep, body, 0.0))
-            for p in range(TILES):
-                above = jnp.where(outside[0], 0.0, row_in[fold, 0, par, p])
-                below = jnp.where(outside[1], 0.0, row_in[fold, 1, par, p])
-                zeros = jnp.zeros((PAIRS - 16, 128), F32)
-                value = acc[par, p + 1, 8:72] + jnp.concatenate([above, zeros, below], axis=0)
-                if p == 0:
-                    value = value + adds[0]
-                if p + 1 == TILES:
-                    value = value + adds[1]
+                value = value - ((m1 - above) + (m2 - before))
                 old = x_v[par, p]
                 new = old - TAU * value
                 x_v[par, p] = new
                 bar_v[par, p] = 2.0 * new - old
+        if step + 1 == ITERS:
+            for par in (0, 1):
+                for p in range(TILES):
+                    dual_out_ref[p, pl.ds(par, PAIRS, stride=2), :] = y_v[par, p]
+
+        wait_in(fold)
+
+        def subtract(par, p, a, b, value):
+            x_v[par, p, a:b] = x_v[par, p, a:b] - TAU * value
+            bar_v[par, p, a:b] = bar_v[par, p, a:b] - 2.0 * TAU * value
+
+        for par in (0, 1):
+            for s, p, first_lane in ((0, 0, 0), (1, TILES - 1, 112)):
+                message = jnp.where(outside[2 + s], 0.0, col_in[fold, s])
+                keep = lane16 < 15 if s == 0 else lane16 >= 113
+                for k in range(4):
+                    value = jnp.where(keep, unpacked(message, 4 * par + k, first_lane), 0.0)
+                    subtract(par, p, 16 * k, 16 * k + 16, value)
+            for d, (a, b) in ((0, (0, 8)), (1, (PAIRS - 8, PAIRS))):
+                for p in range(TILES):
+                    value = jnp.where(outside[d], 0.0, row_in[fold, d, par, p])
+                    if p in (0, TILES - 1):
+                        s = 0 if p == 0 else 1
+                        message = jnp.where(outside[4 + 2 * d + s], 0.0, cor_in[fold, 2 * d + s])
+                        keep = lane8 < 15 if s == 0 else lane8 >= 113
+                        value = value + jnp.where(keep, unpacked(message, par, 112 * s), 0.0)
+                    subtract(par, p, a, b, value)
         if step + 1 < ITERS:
             send_image(halo + 2)
 
     for par in (0, 1):
         for p in range(TILES):
-            rows_of = pl.ds(par, PAIRS, stride=2)
-            restored_ref[p, rows_of, :] = x_v[par, p]
-            dual_out_ref[p, rows_of, :] = y_v[par, p]
+            restored_ref[p, pl.ds(par, PAIRS, stride=2), :] = x_v[par, p]
     for exchange in range(2 * ITERS):
         wait_out(exchange)
 
@@ -433,18 +500,20 @@
             pltpu.VMEM(tiled, F32),
             pltpu.VMEM(tiled, F32),
             pltpu.VMEM((2,) + tiled, F32),
-            pltpu.VMEM((4, 64, 128), F32),
+            pltpu.VMEM((8, 64, 128), F32),
             pltpu.VMEM((TILES * 4096, 128), BF16),
+            pltpu.VMEM((TILES * T_ROWS, 256), BF16),
             pltpu.VMEM(block, F32),
             pltpu.VMEM(block, F32),
             pltpu.VMEM(block, F32),
             pltpu.VMEM(block, F32),
             pltpu.VMEM(block, F32),
             pltpu.VMEM(block, F32),
-            pltpu.VMEM((2, 2, TILES, 88, 128), F32),
+            pltpu.VMEM((2, 2, TILES, 80, 128), F32),
+            pltpu.VMEM((2, 2, TILES, 80, 128), F32),
+            pltpu.VMEM((TILES, 128, 128), F32),
             pltpu.VMEM((2, TILES, 96, 128), F32),
             pltpu.VMEM((2, 2, TILES, 88, 128), F32),
-            pltpu.VMEM((2, TILES + 2, 80, 128), F32),
             pltpu.VMEM((exchanges, 2, 2, TILES, 8, 128), F32),
             pltpu.VMEM((exchanges, 2, 16, 128), F32),
             pltpu.VMEM((exchanges, 4, 8, 128), F32),

time: 36.8 us -> 29.5 us (0.80)
  Pallas kernels: 36 us -> 28.7 us
    pallas_call x1, Pallas kernels: 35.2 us -> 27.9 us  [per_device(): pl.pallas_call(kernel, out_shape=(pltpu.VMEM(tiled, F32), pltpu.VMEM(tile...]
where the time goes in v3:
time: 29.5 us; the launch traced here: 29.4 us
  Pallas kernels  28.7 us (97%)
  between operations  0.64 us (2%)
    pallas_call x1, Pallas kernels, per_device(): pl.pallas_call(kernel, out_shape=(pltpu.VMEM(tiled, F32), pltpu.VMEM(tile...  27.9 us
    pallas_call x1, Pallas kernels, per_device(): pl.pallas_call(put_out, out_shape=(jax.ShapeDtypeStruct(shape, F32), jax....  0.85 us

profile of v3, /device:TPU:27, one launch (start us, length us, event | category | flops | bytes accessed | tf_op | source)
XLA Modules:
  0.0 29.4 jit_solution(10484774274280044850)
XLA Ops:
  0.6 27.9 %shard_map.77 = (f32[4,128,128]{2,1,0:T(8,128)S(1)}, f32[4,128,128]{2,1,0:T(8,128)S(1)}) custom-call(s32[1,4]{1,0:T(1,128)} %index_ref.1, f32[128,512]{1,0:T(8,128)} %observed_hbm.1, bf16[31,31,64]{2,1,0:T(8,128)(2,1)} %bitcast.1, f32[128,512]{1,0:T(8,128)} %start_hbm.1, f32[128,512]{1,0:T(8,128)} %dual_hbm.1, f32[2,128,512]{2,1,0:T(8,128)} %tv_hbm.1), custom_call_target="tpu_custom_call" | custom-call | tf_op jit(solution)/shard_map/pallas_call | solution.py:492
  28.5 0.9 %shard_map.78 = (f32[128,512]{1,0:T(8,128)}, f32[128,512]{1,0:T(8,128)}) custom-call(f32[4,128,128]{2,1,0:T(8,128)S(1)} %get-tuple-element.4.restored_ref, f32[4,128,128]{2,1,0:T(8,128)S(1)} %get-tuple-element.5.dual_ref), custom_call_target="tpu_custom_call" | custom-call | tf_op jit(solution)/shard_map/pallas_call | solution.py:529

commit v4 on v3

v4 whole, which is shorter than its diff:
```python
import jax
import jax.numpy as jnp
from jax import lax
from jax.experimental import pallas as pl
from jax.experimental.pallas import tpu as pltpu
from jax.sharding import PartitionSpec as P

EXCHANGES = 3
SIGMA = 0.15
TAU = 0.6
WEIGHT = 0.5
TAPS = 31
PAIRS = 64
TILES = 4
DIRS = ((-1, 0), (1, 0), (0, -1), (0, 1), (-1, -1), (-1, 1), (1, -1), (1, 1))
OPPOSITE = (1, 0, 3, 2, 7, 6, 5, 4)
MESH_ID = pl.DeviceIdType.MESH
F32 = jnp.float32
BF16 = jnp.bfloat16


def lanes(shape):
    return lax.broadcasted_iota(jnp.int32, shape, 1)


def roll(value, shift):
    shift = shift % 128
    return value if shift == 0 else pltpu.roll(value, shift, 1)


T_ROWS = 17 * 128


def kernel(
    index_hbm, observed_hbm, table_hbm, start_hbm, dual_hbm, tv_hbm,
    restored_ref, dual_out_ref,
    start_v, table_v, index_ref, observed_v, dual_v, tv_v,
    base_v, weights, weights_t, x_e, bar_e, acc, obs_v, y_v, q1_v, q2_v, shifted, shifted_halo, blur_v, ypad, spread,
    row_out, col_out, cor_out, row_in, col_in, cor_in,
    wide_row_out, wide_col_out, wide_cor_out, wide_row_in, wide_col_in, wide_cor_in,
    load_sem, send_sem, recv_sem,
):
    row, col = lax.axis_index("row"), lax.axis_index("col")
    rows, cols = lax.axis_size("row"), lax.axis_size("col")

    def at(direction):
        dr, dc = direction
        return (lax.rem(row + dr + rows, rows), lax.rem(col + dc + cols, cols))

    top, bottom = row == 0, row == rows - 1
    left, right = col == 0, col == cols - 1
    outside = (top, bottom, left, right, top | left, top | right, bottom | left, bottom | right)
    inside = [jnp.logical_not(o) for o in outside]

    barrier = pltpu.get_barrier_semaphore()
    for d, direction in enumerate(DIRS):
        @pl.when(inside[d])
        def _():
            pl.semaphore_signal(barrier, inc=1, device_id=at(direction), device_id_type=MESH_ID)

    slices = [slice(128 * p, 128 * p + 128) for p in range(TILES)]
    plain = ((start_hbm, start_v), (observed_hbm, observed_v), (dual_hbm, dual_v))
    sources = [(src.at[:, slices[p]], dst.at[p]) for src, dst in plain for p in range(TILES)]
    sources += [(tv_hbm.at[:, :, slices[p]], tv_v.at[:, p]) for p in range(TILES)]
    sources[TILES:TILES] = [(table_hbm, table_v), (index_hbm, index_ref)]
    loads = [pltpu.make_async_copy(src, dst, load_sem.at[i]) for i, (src, dst) in enumerate(sources)]
    for load in loads:
        load.start()

    lane64 = lanes((PAIRS, 128))
    lane8 = lanes((8, 128))
    lane16 = lanes((16, 128))

    wide = (wide_row_out, wide_col_out, wide_cor_out, wide_row_in, wide_col_in, wide_cor_in)
    narrow = (row_out, col_out, cor_out, row_in, col_in, cor_in)

    def copies(exchange):
        refs = wide if exchange == 1 else [ref.at[exchange // 2] for ref in narrow]
        result = []
        for d, direction in enumerate(DIRS):
            if d < 2:
                src, dst = refs[0].at[d], refs[3].at[d ^ 1]
            elif d < 4:
                src, dst = refs[1].at[d - 2], refs[4].at[(d - 2) ^ 1]
            else:
                src, dst = refs[2].at[d - 4], refs[5].at[3 - (d - 4)]
            back = OPPOSITE[d]
            result.append(
                pltpu.make_async_remote_copy(
                    src_ref=src,
                    dst_ref=dst,
                    send_sem=send_sem.at[exchange, d],
                    recv_sem=recv_sem.at[exchange, back],
                    device_id=at(direction),
                    device_id_type=MESH_ID,
                )
            )
        return result

    def start_out(exchange):
        for d, copy in enumerate(copies(exchange)):
            pl.when(inside[d])(copy.start)

    def wait_in(exchange):
        for d, copy in enumerate(copies(exchange)):
            pl.when(inside[OPPOSITE[d]])(copy.wait_recv)

    def wait_out(exchange):
        for d, copy in enumerate(copies(exchange)):
            pl.when(inside[d])(copy.wait_send)

    def packed(parts, first_lane, height):
        lane = lane16 if height == 16 else lane8
        message = None
        for f, part in enumerate(parts):
            moved = roll(part, 16 * f - first_lane)
            message = moved if f == 0 else jnp.where(lane >= 16 * f, moved, message)
        return message

    def unpacked(message, f, first_lane):
        return roll(message, first_lane - 16 * f)

    x_e[...] = jnp.zeros_like(x_e)
    bar_e[...] = jnp.zeros_like(bar_e)
    for load in loads[:TILES]:
        load.wait()
    for par in (0, 1):
        for p in range(TILES):
            value = start_v[p, pl.ds(par, PAIRS, stride=2), :]
            x_e[par, p + 1, 8:72] = value
            bar_e[par, p + 1, 8:72] = value
    for d, first in ((0, 8), (1, 64)):
        for par in (0, 1):
            for p in range(TILES):
                row_out[0, d, par, p] = bar_e[par, p + 1, first : first + 8]
    for s, (q, first_lane) in enumerate(((1, 0), (TILES, 112))):
        col_out[0, s] = packed(
            [bar_e[par, q, 8 + 16 * k : 24 + 16 * k] for par in (0, 1) for k in range(4)], first_lane, 16
        )
        for d, first in ((0, 8), (1, 64)):
            cor_out[0, 2 * d + s] = packed([bar_e[par, q, first : first + 8] for par in (0, 1)], first_lane, 8)

    pl.semaphore_wait(barrier, sum(i.astype(jnp.int32) for i in inside))
    start_out(0)

    for load in loads[TILES : TILES + 2]:
        load.wait()
    which = lax.broadcasted_iota(jnp.int32, (8, 64), 0) & 3
    entry = lanes((8, 64))
    chosen = jnp.zeros((8, 64), F32)
    for p in range(TILES):
        chosen = jnp.where((which == p) & (entry == index_ref[0, p]), 1.0, chosen)
    chosen = chosen.astype(BF16)
    gap = jnp.zeros((1, 64), F32)
    lines = [
        jnp.concatenate([table_v[a].astype(F32), gap], axis=0).astype(BF16)
        if a < TAPS else jnp.zeros((32, 64), BF16)
        for a in range(32)
    ]
    picked = jnp.concatenate(
        [
            lax.dot_general(
                chosen,
                jnp.concatenate(lines[8 * k : 8 * k + 8], axis=0),
                (((1,), (1,)), ((), ())),
                preferred_element_type=F32,
            )
            for k in range(4)
        ],
        axis=1,
    )
    normed = picked / jnp.sum(picked, axis=1, keepdims=True)
    kernels = jnp.concatenate([normed[:, 128 * q : 128 * q + 128] for q in range(8)], axis=0)
    before = jnp.concatenate([jnp.zeros((8, 128), F32), kernels[:56]], axis=0)
    kernels, before = kernels.astype(BF16), before.astype(BF16)
    tap = lax.broadcasted_iota(jnp.int32, (128, 128), 0)
    place = lanes((128, 128))

    def flip(r, first):
        hit = ((tap >> 5) == r) & (place == ((first - (tap & 31)) & 127))
        return hit.astype(F32).astype(BF16)

    lane_of = lanes((64, 128))
    for r in range(4):
        low = jnp.dot(kernels, flip(r, 128), preferred_element_type=F32)
        high = jnp.dot(kernels if r else before, flip((r - 1) & 3, 64), preferred_element_type=F32)
        base_v[r] = low + high
        base_v[4 + r] = jnp.where(lane_of < 32, roll(kernels.astype(F32), -32 * r), 0.0)
    reach = tap - (place & 63)
    band = (reach >= 0) & (reach < TAPS)
    for p in range(TILES):
        weights_t[p * T_ROWS + 64 : p * T_ROWS + 128, 0:128] = jnp.zeros((64, 128), BF16)

    def build(q, carry):
        for p in range(TILES):
            for r in range(4):
                line = base_v[r, pl.ds(q * 8 + p, 1), :]
                rolled = pltpu.roll(jnp.broadcast_to(line, (128, 128)), 0, 1, stride=1, stride_axis=0)
                start = pl.multiple_of(p * 4096 + (q * 4 + r) * 128, 128)
                weights[pl.ds(start, 128), :] = jnp.where(band, rolled, 0.0).astype(BF16)
                line = base_v[4 + r, pl.ds(q * 8 + p, 1), :]
                rolled = pltpu.roll(jnp.broadcast_to(line, (64, 128)), 0, 1, stride=1, stride_axis=0).astype(BF16)
                for d in (0, 1):
                    t, e = (r + d) >> 1, (r + d) & 1
                    start = pl.multiple_of(p * T_ROWS + (q * 2 + t) * 128 + d * 64, 64)
                    weights_t[pl.ds(start, 64), 128 * e : 128 * e + 128] = rolled
        return carry

    lax.fori_loop(0, 8, build, 0)

    ypad[...] = jnp.zeros_like(ypad)
    shifted[...] = jnp.zeros_like(shifted)
    shifted_halo[...] = jnp.zeros_like(shifted_halo)
    for h in (0, 1):
        for p in range(TILES):
            spread[0, h, p, 0:8] = jnp.zeros((8, 128), F32)
    for load in loads[TILES + 2 :]:
        load.wait()
    for par in (0, 1):
        for p in range(TILES):
            rows_of = pl.ds(par, PAIRS, stride=2)
            obs_v[par, p] = observed_v[p, rows_of, :]
            y_v[par, p] = dual_v[p, rows_of, :]
            q1_v[par, p] = tv_v[0, p, rows_of, :]
            q2_v[par, p] = tv_v[1, p, rows_of, :]

    def stacked_rows(source, p, ranges):
        pieces = []
        for t in range(16):
            for par in (1, 0):
                first = t + 1 - par
                pieces.append(
                    jnp.concatenate(
                        [source[par, h, p, a + first : a + first + n] for h, a, n in ranges], axis=0
                    ).astype(BF16)
                )
        return jnp.concatenate(pieces, axis=1)

    def lay(target, par, a, b):
        lane = lanes((b - a, 128))
        tiles = [bar_e[par, q, a:b] for q in range(TILES + 2)]
        by15 = [roll(t, 15) for t in tiles[:-1]]
        by79 = [roll(t, 79) for t in tiles[1:]]
        for p in range(TILES):
            target[par, 0, p, a:b] = jnp.where(lane < 15, by15[p], by15[p + 1])
            target[par, 1, p, a:b] = jnp.where(lane < 79, by79[p], by79[p + 1])

    def lay_sides(par, a, b, reach_in):
        lane = lanes((b - a, 128))
        first = jnp.where(lane < 15, roll(bar_e[par, 0, a:b], 15), roll(bar_e[par, 1, a:b], 15))
        last = jnp.where(lane < 79, roll(bar_e[par, TILES, a:b], 79), roll(bar_e[par, TILES + 1, a:b], 79))
        shifted_halo[par, 0, 0, a:b] = jnp.where(lane < 15 + reach_in, first, 0.0)
        shifted_halo[par, 1, TILES - 1, a:b] = jnp.where(lane >= 79 - reach_in, last, 0.0)

    def blur_own(p, carry):
        lhs = stacked_rows(shifted, p, ((0, 0, PAIRS), (1, 0, PAIRS)))
        matrix = weights[pl.ds(pl.multiple_of(p * 4096, 4096), 4096), :]
        blur_v[p] = jnp.dot(lhs, matrix, preferred_element_type=F32)
        return carry

    def tv(par, p, a, b):
        value = bar_e[par, p + 1, a + 8 : b + 8]
        if par == 0:
            grad1 = bar_e[1, p + 1, a + 8 : b + 8] - value
        else:
            grad1 = bar_e[0, p + 1, a + 9 : b + 9] - value
            if b == PAIRS:
                grad1 = jnp.where(
                    (lax.broadcasted_iota(jnp.int32, (b - a, 128), 0) == b - a - 1) & bottom, 0.0, grad1
                )
        lane = lanes((b - a, 128))
        grad2 = jnp.where(lane < 127, roll(value, 127), roll(bar_e[par, p + 2, a + 8 : b + 8], 127)) - value
        if p + 1 == TILES:
            grad2 = jnp.where((lane == 127) & right, 0.0, grad2)
        u1 = q1_v[par, p, a:b] + SIGMA * grad1
        u2 = q2_v[par, p, a:b] + SIGMA * grad2
        shrink = jnp.maximum(1.0, jnp.sqrt(u1 * u1 + u2 * u2) / WEIGHT)
        q1_v[par, p, a:b] = u1 / shrink
        q2_v[par, p, a:b] = u2 / shrink

    def merged(par, q, a, b):
        lane = lanes((b - a, 128))
        if q == 0:
            value = spread[par, 0, 0, a:b] + jnp.where(lane >= 64, roll(spread[par, 1, 0, a:b], 64), 0.0)
        elif q == TILES:
            value = jnp.where(lane < 64, roll(spread[par, 1, q - 1, a:b], 64), 0.0)
        else:
            value = spread[par, 0, q, a:b] + jnp.where(
                lane >= 64, roll(spread[par, 1, q, a:b], 64), roll(spread[par, 1, q - 1, a:b], 64)
            )
        return roll(value, 113)

    def own_part(par, p, a, b, tiles):
        lane = lanes((b - a, 128))
        sub = lax.broadcasted_iota(jnp.int32, (b - a, 128), 0)
        i, j = a - 8, b - 8
        m1, m2 = q1_v[par, p, i:j], q2_v[par, p, i:j]
        if par == 1:
            above = q1_v[0, p, i:j]
            if b == 72:
                m1 = jnp.where((sub == b - a - 1) & bottom, 0.0, m1)
        elif a == 8:
            above = jnp.concatenate([jnp.zeros((1, 128), F32), q1_v[1, p, : j - 1]], axis=0)
        else:
            above = q1_v[1, p, i - 1 : j - 1]
        outer = roll(q2_v[par, p - 1, i:j], 1) if p else 0.0
        before = jnp.where(lane == 0, outer, roll(m2, 1))
        if p + 1 == TILES:
            m2 = jnp.where((lane == 127) & right, 0.0, m2)
        return jnp.where(lane < 113, tiles[p], tiles[p + 1]) - ((m1 - above) + (m2 - before))

    def rim_part(par, p, d, tiles):
        value = jnp.where(lane8 < 113, tiles[p], tiles[p + 1])
        if d == 1 and par == 0:
            edge = jnp.concatenate([q1_v[1, p, PAIRS - 1 : PAIRS], jnp.zeros((7, 128), F32)], axis=0)
            value = value + edge
        return value

    def side_part(par, s, a, b, tile):
        lane = lanes((b - a, 128))
        if s == 0:
            return jnp.where(lane >= 113, tile, 0.0)
        value = jnp.where(lane < 15, tile, 0.0)
        if 8 <= a < 72:
            value = value + jnp.where(lane == 0, roll(q2_v[par, TILES - 1, a - 8 : b - 8], 1), 0.0)
        return value

    def masked(direction, value):
        return jnp.where(outside[direction], 0.0, value)

    def duals(edge):
        gap = jnp.zeros((PAIRS - 2 * edge, 128), F32)

        def rows_full(p):
            return 0 if p == 0 else 1 if p + 1 == TILES else None

        def blur_halo(p):
            full = rows_full(p)
            ranges = [(full, 0, PAIRS)] if full is not None else []
            for h in (0, 1):
                if h != full:
                    ranges += [(h, 0, edge), (h, PAIRS - edge, edge)]
            return jnp.dot(
                stacked_rows(shifted_halo, p, ranges),
                weights[p * 4096 : p * 4096 + 4096],
                preferred_element_type=F32,
            )

        def dual(p, extra):
            full = rows_full(p)
            halves, place_r = [None, None], 0
            if full is not None:
                halves[full] = blur_v[p, PAIRS * full : PAIRS * full + PAIRS] + extra[:PAIRS]
                place_r = PAIRS
            for h in (0, 1):
                if h != full:
                    more = jnp.concatenate(
                        [extra[place_r : place_r + edge], gap, extra[place_r + edge : place_r + 2 * edge]], axis=0
                    )
                    halves[h] = blur_v[p, PAIRS * h : PAIRS * h + PAIRS] + more
                    place_r += 2 * edge
            even = jnp.where(lane64 < 64, halves[0], roll(halves[1], 64))
            odd = jnp.where(lane64 < 64, roll(halves[0], 64), halves[1])
            new = []
            for par, value in ((0, even), (1, odd)):
                updated = (y_v[par, p] + SIGMA * (value - obs_v[par, p])) / (1.0 + SIGMA)
                y_v[par, p] = updated
                new.append(updated)
            ypad[0, p, 16 : 16 + PAIRS] = jnp.where(lane64 < 64, new[0], roll(new[1], 64))
            ypad[1, p, 16 : 16 + PAIRS] = jnp.where(lane64 < 64, roll(new[0], 64), new[1])

        def adjoint(p):
            out = jnp.dot(
                jnp.concatenate(
                    [
                        jnp.concatenate([ypad[h, p, 16 - t : 96 - t] for h in (0, 1)], axis=0).astype(BF16)
                        for t in range(16)
                    ],
                    axis=1,
                ),
                weights_t[p * T_ROWS : p * T_ROWS + 2048],
                preferred_element_type=F32,
            )
            for h in (0, 1):
                spread[1, h, p, 0:80] = out[80 * h : 80 * h + 80, 0:128]
                spread[0, h, p, 1:81] = out[80 * h : 80 * h + 80, 128:256]

        extras = [blur_halo(p) for p in range(TILES)]
        for p in range(TILES):
            dual(p, extras[p])
        for p in range(TILES):
            adjoint(p)

    for par in (0, 1):
        lay(shifted, par, 8, 72)
    lax.fori_loop(0, TILES, blur_own, 0)
    for p in range(TILES - 1):
        tv(0, p, 0, PAIRS)
        tv(1, p, 0, PAIRS - 8)

    wait_in(0)
    for par in (0, 1):
        for d, (a, b) in ((0, (0, 8)), (1, (72, 80))):
            for p in range(TILES):
                value = masked(d, row_in[0, d, par, p])
                x_e[par, p + 1, a:b] = value
                bar_e[par, p + 1, a:b] = value
            for s, q in ((0, 0), (1, TILES + 1)):
                value = masked(4 + 2 * d + s, unpacked(cor_in[0, 2 * d + s], par, 112 - 112 * s))
                x_e[par, q, a:b] = value
                bar_e[par, q, a:b] = value
        for s, q in ((0, 0), (1, TILES + 1)):
            for k in range(4):
                value = masked(2 + s, unpacked(col_in[0, s], 4 * par + k, 112 - 112 * s))
                x_e[par, q, 8 + 16 * k : 24 + 16 * k] = value
                bar_e[par, q, 8 + 16 * k : 24 + 16 * k] = value
        lay(shifted_halo, par, 0, 8)
        lay(shifted_halo, par, 72, 80)
        lay_sides(par, 8, 72, 0)

    duals(8)
    for p in range(TILES - 1):
        tv(1, p, PAIRS - 8, PAIRS)
    for par in (0, 1):
        tv(par, TILES - 1, 0, PAIRS)

    for par in (0, 1):
        for d, first in ((0, 0), (1, 64)):
            for a, b in ((first, first + 8), (first + 8, first + 16)):
                own = 8 <= a < 72
                tiles = [merged(par, q, a, b) for q in range(TILES + 1)]
                for p in range(TILES):
                    value = own_part(par, p, a, b, tiles) if own else rim_part(par, p, d, tiles)
                    acc[par, p + 1, a:b] = value
                    wide_row_out[d, TILES * par + p, a - first : b - first] = value
                acc[par, 0, a:b] = side_part(par, 0, a, b, tiles[0])
                acc[par, TILES + 1, a:b] = side_part(par, 1, a, b, tiles[TILES])
        a, b = 16, 64
        tiles = [merged(par, q, a, b) if q != 2 else None for q in range(TILES + 1)]
        for p in (0, TILES - 1):
            acc[par, p + 1, a:b] = own_part(par, p, a, b, tiles)
        acc[par, 0, a:b] = side_part(par, 0, a, b, tiles[0])
        acc[par, TILES + 1, a:b] = side_part(par, 1, a, b, tiles[TILES])
    for d, first in ((0, 0), (1, 64)):
        message = None
        for f, (par, s) in enumerate(((0, 0), (0, 1), (1, 0), (1, 1))):
            moved = roll(acc[par, (TILES + 1) * s, first : first + 16], 16 * f - 112 + 112 * s)
            message = moved if f == 0 else jnp.where(lane16 >= 16 * f, moved, message)
        wide_row_out[d, 2 * TILES] = message
    for s, q in ((0, 0), (1, TILES)):
        around = [
            jnp.where(lanes((80, 128)) < 16, roll(acc[par, q], 16), roll(acc[par, q + 1], 16)) for par in (0, 1)
        ]
        message = None
        for f in range(4):
            moved = roll(around[f >> 1][40 * (f & 1) : 40 * (f & 1) + 40], 32 * f)
            message = moved if f == 0 else jnp.where(lanes((40, 128)) >= 32 * f, moved, message)
        wide_col_out[s] = message
        for d, first in ((0, 0), (1, 64)):
            message = None
            for f in range(4):
                start = first + 8 * (f & 1)
                moved = roll(around[f >> 1][start : start + 8], 32 * f)
                message = moved if f == 0 else jnp.where(lane8 >= 32 * f, moved, message)
            wide_cor_out[2 * d + s] = message
    start_out(1)

    for par in (0, 1):
        a, b = 16, 64
        tiles = [None] + [merged(par, q, a, b) for q in (1, 2, 3)] + [None]
        for p in range(TILES):
            value = own_part(par, p, a, b, tiles) if p in (1, 2) else acc[par, p + 1, a:b]
            old = x_e[par, p + 1, a:b]
            new = old - TAU * value
            x_e[par, p + 1, a:b] = new
            bar_e[par, p + 1, a:b] = 2.0 * new - old
        lay(shifted, par, a, b)
        lane = lanes((b - a, 128))
        shifted[par, 0, 0, a:b] = jnp.where(lane < 30, 0.0, shifted[par, 0, 0, a:b])
        shifted[par, 1, TILES - 1, a:b] = jnp.where(lane >= 64, 0.0, shifted[par, 1, TILES - 1, a:b])
        for h in (0, 1):
            for p in range(TILES):
                shifted[par, h, p, 8:16] = jnp.zeros((8, 128), F32)
                shifted[par, h, p, 64:72] = jnp.zeros((8, 128), F32)
    lax.fori_loop(0, TILES, blur_own, 0)
    for p in (1, 2):
        tv(0, p, 8, 56)
        tv(1, p, 8, 48)

    wait_in(1)
    for par in (0, 1):
        beside = []
        for s in (0, 1):
            halves = [masked(2 + s, wide_col_in[s]) for _ in (0, 1)]
            lane = lanes((40, 128))
            low = [jnp.where(lane >= 112, roll(halves[k], 112 - 32 * (2 * par + k)), 0.0) for k in (0, 1)]
            high = [jnp.where(lane < 16, roll(halves[k], -16 - 32 * (2 * par + k)), 0.0) for k in (0, 1)]
            beside.append((jnp.concatenate(low, axis=0), jnp.concatenate(high, axis=0)))
        for a, b in ((16, 64),):
            for s, q in ((0, 0), (1, TILES)):
                for k in (0, 1):
                    more = beside[s][k][a:b]
                    old = x_e[par, q + k, a:b]
                    if q + k in (0, TILES + 1):
                        value = acc[par, q + k, a:b] + more
                        new = old - TAU * value
                        bar_e[par, q + k, a:b] = masked(2 + s, 2.0 * new - old)
                    else:
                        x_e[par, q + k, a:b] = old - TAU * more
                        bar_e[par, q + k, a:b] = bar_e[par, q + k, a:b] - 2.0 * TAU * more
        for d, first in ((0, 0), (1, 64)):
            for k8 in (0, 1):
                a, b = first + 8 * k8, first + 8 * k8 + 8
                for q in range(TILES + 2):
                    value = acc[par, q, a:b]
                    if 1 <= q <= TILES:
                        value = value + masked(d, wide_row_in[d, TILES * par + q - 1, 8 * k8 : 8 * k8 + 8])
                    else:
                        s = 0 if q == 0 else 1
                        f = 2 * par + s
                        more = roll(wide_row_in[d, 2 * TILES, 8 * k8 : 8 * k8 + 8], 112 - 112 * s - 16 * f)
                        value = value + masked(d, jnp.where((lane8 >= 112) if s == 0 else (lane8 < 16), more, 0.0))
                    for s, line in ((0, 0), (1, TILES)):
                        if q in (line, line + 1):
                            message = wide_cor_in[2 * d + s]
                            f = 2 * par + k8
                            if q == line:
                                more = jnp.where(lane8 >= 112, roll(message, 112 - 32 * f), 0.0)
                            else:
                                more = jnp.where(lane8 < 16, roll(message, -16 - 32 * f), 0.0)
                            value = value + beside[s][q - line][a:b] + masked(4 + 2 * d + s, more)
                    old = x_e[par, q, a:b]
                    new = old - TAU * value
                    bar = 2.0 * new - old
                    if q == 0:
                        bar = masked(2, bar)
                    if q == TILES + 1:
                        bar = masked(3, bar)
                    if not 8 <= a < 72:
                        bar = masked(d, bar)
                    x_e[par, q, a:b] = new
                    bar_e[par, q, a:b] = bar
        lay(shifted_halo, par, 0, 16)
        lay(shifted_halo, par, 64, 80)
        lay_sides(par, 16, 64, 15)

    duals(16)
    for p in (1, 2):
        tv(0, p, 0, 8)
        tv(0, p, 56, 64)
        tv(1, p, 0, 8)
        tv(1, p, 48, 64)
    for par in (0, 1):
        for p in (0, TILES - 1):
            tv(par, p, 0, PAIRS)

    corners = [[None, None] for _ in range(4)]
    for par in (0, 1):
        for d, (a, b) in ((0, (0, 8)), (1, (72, 80))):
            tiles = [merged(par, q, a, b) for q in range(TILES + 1)]
            for p in range(TILES):
                row_out[1, d, par, p] = rim_part(par, p, d, tiles)
            for s in (0, 1):
                corners[2 * d + s][par] = side_part(par, s, a, b, tiles[TILES * s])
    for s, first_lane in ((0, 112), (1, 0)):
        side = [side_part(par, s, 8, 72, merged(par, TILES * s, 8, 72)) for par in (0, 1)]
        col_out[1, s] = packed([side[par][16 * k : 16 * k + 16] for par in (0, 1) for k in range(4)], first_lane, 16)
        for d in (0, 1):
            cor_out[1, 2 * d + s] = packed(corners[2 * d + s], first_lane, 8)
    start_out(2)

    for par in (0, 1):
        tiles = [merged(par, q, 8, 72) for q in range(TILES + 1)]
        for p in range(TILES):
            x_e[par, p + 1, 8:72] = x_e[par, p + 1, 8:72] - TAU * own_part(par, p, 8, 72, tiles)
            dual_out_ref[p, pl.ds(par, PAIRS, stride=2), :] = y_v[par, p]

    wait_in(2)

    def subtract(par, q, a, b, value):
        x_e[par, q, a:b] = x_e[par, q, a:b] - TAU * value

    for par in (0, 1):
        for s, q, first_lane in ((0, 1, 0), (1, TILES, 112)):
            message = masked(2 + s, col_in[1, s])
            keep = lane16 < 15 if s == 0 else lane16 >= 113
            for k in range(4):
                value = jnp.where(keep, unpacked(message, 4 * par + k, first_lane), 0.0)
                subtract(par, q, 8 + 16 * k, 24 + 16 * k, value)
        for d, (a, b) in ((0, (8, 16)), (1, (64, 72))):
            for p in range(TILES):
                value = masked(d, row_in[1, d, par, p])
                if p in (0, TILES - 1):
                    s = 0 if p == 0 else 1
                    message = masked(4 + 2 * d + s, cor_in[1, 2 * d + s])
                    keep = lane8 < 15 if s == 0 else lane8 >= 113
                    value = value + jnp.where(keep, unpacked(message, par, 112 * s), 0.0)
                subtract(par, p + 1, a, b, value)
    for par in (0, 1):
        for p in range(TILES):
            restored_ref[p, pl.ds(par, PAIRS, stride=2), :] = x_e[par, p + 1, 8:72]
    for exchange in range(EXCHANGES):
        wait_out(exchange)


def put_out(restored_ref, dual_ref, restored_hbm, dual_hbm, store_sem):
    stores = [
        pltpu.make_async_copy(src.at[p], dst.at[:, 128 * p : 128 * p + 128], store_sem.at[TILES * i + p])
        for i, (src, dst) in enumerate(((restored_ref, restored_hbm), (dual_ref, dual_hbm)))
        for p in range(TILES)
    ]
    for store in stores:
        store.start()
    for store in stores:
        store.wait()


def per_device(observed, psf_table, psf_index, start_image, blur_dual, tv_dual):
    shape = observed.shape
    block = (2, TILES, PAIRS, 128)
    extended = (2, TILES + 2, 80, 128)
    tiled = (TILES, 2 * PAIRS, 128)
    hbm = pl.BlockSpec(memory_space=pl.ANY)
    table = psf_table.transpose(1, 2, 0)
    results = pl.pallas_call(
        kernel,
        out_shape=(pltpu.VMEM(tiled, F32), pltpu.VMEM(tiled, F32)),
        in_specs=[hbm] * 6,
        out_specs=(pl.BlockSpec(memory_space=pltpu.VMEM),) * 2,
        scratch_shapes=[
            pltpu.VMEM(tiled, F32),
            pltpu.VMEM(table.shape, BF16),
            pltpu.SMEM(psf_index.shape, jnp.int32),
            pltpu.VMEM(tiled, F32),
            pltpu.VMEM(tiled, F32),
            pltpu.VMEM((2,) + tiled, F32),
            pltpu.VMEM((8, 64, 128), F32),
            pltpu.VMEM((TILES * 4096, 128), BF16),
            pltpu.VMEM((TILES * T_ROWS, 256), BF16),
            pltpu.VMEM(extended, F32),
            pltpu.VMEM(extended, F32),
            pltpu.VMEM(extended, F32),
            pltpu.VMEM(block, F32),
            pltpu.VMEM(block, F32),
            pltpu.VMEM(block, F32),
            pltpu.VMEM(block, F32),
            pltpu.VMEM((2, 2, TILES, 80, 128), F32),
            pltpu.VMEM((2, 2, TILES, 80, 128), F32),
            pltpu.VMEM((TILES, 128, 128), F32),
            pltpu.VMEM((2, TILES, 96, 128), F32),
            pltpu.VMEM((2, 2, TILES, 88, 128), F32),
            pltpu.VMEM((2, 2, 2, TILES, 8, 128), F32),
            pltpu.VMEM((2, 2, 16, 128), F32),
            pltpu.VMEM((2, 4, 8, 128), F32),
            pltpu.VMEM((2, 2, 2, TILES, 8, 128), F32),
            pltpu.VMEM((2, 2, 16, 128), F32),
            pltpu.VMEM((2, 4, 8, 128), F32),
            pltpu.VMEM((2, 2 * TILES + 1, 16, 128), F32),
            pltpu.VMEM((2, 40, 128), F32),
            pltpu.VMEM((4, 8, 128), F32),
            pltpu.VMEM((2, 2 * TILES + 1, 16, 128), F32),
            pltpu.VMEM((2, 40, 128), F32),
            pltpu.VMEM((4, 8, 128), F32),
            pltpu.SemaphoreType.DMA((4 * TILES + 2,)),
            pltpu.SemaphoreType.DMA((EXCHANGES, 8)),
            pltpu.SemaphoreType.DMA((EXCHANGES, 8)),
        ],
        compiler_params=pltpu.CompilerParams(collective_id=0, has_side_effects=True),
    )(psf_index, observed, table, start_image, blur_dual, tv_dual)
    return pl.pallas_call(
        put_out,
        out_shape=(jax.ShapeDtypeStruct(shape, F32), jax.ShapeDtypeStruct(shape, F32)),
        in_specs=[hbm] * 2,
        out_specs=(hbm, hbm),
        scratch_shapes=[pltpu.SemaphoreType.DMA((2 * TILES,))],
    )(*(pltpu.with_memory_space_constraint(result, pltpu.VMEM) for result in results))


def solution(mesh):
    placed = (
        P("row", "col"),
        P(),
        P("row", "col"),
        P("row", "col"),
        P("row", "col"),
        P(None, "row", "col"),
    )
    return jax.shard_map(
        per_device,
        mesh=mesh,
        in_specs=placed,
        out_specs=(P("row", "col"), P("row", "col")),
        check_vma=False,
    )
```

time: 29.5 us -> 24.7 us (0.84)
  Pallas kernels: 28.7 us -> 23.8 us
    pallas_call x1, Pallas kernels: 27.9 us -> 23 us  [per_device(): pl.pallas_call(kernel, out_shape=(pltpu.VMEM(tiled, F32), pltpu.VMEM(tile...]
where the time goes in v4:
time: 24.7 us; the launch traced here: 24.4 us
  Pallas kernels  23.8 us (96%)
  between operations  0.64 us (3%)
    pallas_call x1, Pallas kernels, per_device(): pl.pallas_call(kernel, out_shape=(pltpu.VMEM(tiled, F32), pltpu.VMEM(tile...  23 us
    pallas_call x1, Pallas kernels, per_device(): pl.pallas_call(put_out, out_shape=(jax.ShapeDtypeStruct(shape, F32), jax....  0.85 us

profile of v4, /device:TPU:27, one launch (start us, length us, event | category | flops | bytes accessed | tf_op | source)
XLA Modules:
  0.0 24.4 jit_solution(426788667165569536)
XLA Ops:
  0.6 23.0 %shard_map.77 = (f32[4,128,128]{2,1,0:T(8,128)S(1)}, f32[4,128,128]{2,1,0:T(8,128)S(1)}) custom-call(s32[1,4]{1,0:T(1,128)} %index_hbm.1, f32[128,512]{1,0:T(8,128)} %observed_hbm.1, bf16[31,31,64]{2,1,0:T(8,128)(2,1)} %bitcast.1, f32[128,512]{1,0:T(8,128)} %start_hbm.1, f32[128,512]{1,0:T(8,128)} %dual_hbm.1, f32[2,128,512]{2,1,0:T(8,128)} %tv_hbm.1), custom_call_target="tpu_custom_call" | custom-call | tf_op jit(solution)/shard_map/pallas_call | solution.py:625
  23.6 0.9 %shard_map.78 = (f32[128,512]{1,0:T(8,128)}, f32[128,512]{1,0:T(8,128)}) custom-call(f32[4,128,128]{2,1,0:T(8,128)S(1)} %get-tuple-element.4.restored_ref, f32[4,128,128]{2,1,0:T(8,128)S(1)} %get-tuple-element.5.dual_ref), custom_call_target="tpu_custom_call" | custom-call | tf_op jit(solution)/shard_map/pallas_call | solution.py:670

commit v5 on v4

--- a/solution.py
+++ b/solution.py
@@ -17,6 +17,7 @@
 MESH_ID = pl.DeviceIdType.MESH
 F32 = jnp.float32
 BF16 = jnp.bfloat16
+STRIP_TYPE = BF16
 
 
 def lanes(shape):
@@ -38,6 +39,7 @@
     base_v, weights, weights_t, x_e, bar_e, acc, obs_v, y_v, q1_v, q2_v, shifted, shifted_halo, blur_v, ypad, spread,
     row_out, col_out, cor_out, row_in, col_in, cor_in,
     wide_row_out, wide_col_out, wide_cor_out, wide_row_in, wide_col_in, wide_cor_in,
+    last_row_out, last_row_in,
     load_sem, send_sem, recv_sem,
 ):
     row, col = lax.axis_index("row"), lax.axis_index("col")
@@ -51,12 +53,6 @@
     left, right = col == 0, col == cols - 1
     outside = (top, bottom, left, right, top | left, top | right, bottom | left, bottom | right)
     inside = [jnp.logical_not(o) for o in outside]
-
-    barrier = pltpu.get_barrier_semaphore()
-    for d, direction in enumerate(DIRS):
-        @pl.when(inside[d])
-        def _():
-            pl.semaphore_signal(barrier, inc=1, device_id=at(direction), device_id_type=MESH_ID)
 
     slices = [slice(128 * p, 128 * p + 128) for p in range(TILES)]
     plain = ((start_hbm, start_v), (observed_hbm, observed_v), (dual_hbm, dual_v))
@@ -64,18 +60,30 @@
     sources += [(tv_hbm.at[:, :, slices[p]], tv_v.at[:, p]) for p in range(TILES)]
     sources[TILES:TILES] = [(table_hbm, table_v), (index_hbm, index_ref)]
     loads = [pltpu.make_async_copy(src, dst, load_sem.at[i]) for i, (src, dst) in enumerate(sources)]
-    for load in loads:
+    for load in loads[:TILES]:
+        load.start()
+
+    barrier = pltpu.get_barrier_semaphore()
+    for d, direction in enumerate(DIRS):
+        @pl.when(inside[d])
+        def _():
+            pl.semaphore_signal(barrier, inc=1, device_id=at(direction), device_id_type=MESH_ID)
+
+    for load in loads[TILES:]:
         load.start()
 
     lane64 = lanes((PAIRS, 128))
     lane8 = lanes((8, 128))
     lane16 = lanes((16, 128))
 
-    wide = (wide_row_out, wide_col_out, wide_cor_out, wide_row_in, wide_col_in, wide_cor_in)
-    narrow = (row_out, col_out, cor_out, row_in, col_in, cor_in)
+    sides = (col_out, cor_out, col_in, cor_in)
+    first_refs = (row_out,) + tuple(ref.at[0] for ref in sides[:2]) + (row_in,) + tuple(ref.at[0] for ref in sides[2:])
+    last_refs = (last_row_out,) + tuple(ref.at[1] for ref in sides[:2])
+    last_refs += (last_row_in,) + tuple(ref.at[1] for ref in sides[2:])
+    wide_refs = (wide_row_out, wide_col_out, wide_cor_out, wide_row_in, wide_col_in, wide_cor_in)
 
     def copies(exchange):
-        refs = wide if exchange == 1 else [ref.at[exchange // 2] for ref in narrow]
+        refs = (first_refs, wide_refs, last_refs)[exchange]
         result = []
         for d, direction in enumerate(DIRS):
             if d < 2:
@@ -120,8 +128,6 @@
     def unpacked(message, f, first_lane):
         return roll(message, first_lane - 16 * f)
 
-    x_e[...] = jnp.zeros_like(x_e)
-    bar_e[...] = jnp.zeros_like(bar_e)
     for load in loads[:TILES]:
         load.wait()
     for par in (0, 1):
@@ -132,7 +138,7 @@
     for d, first in ((0, 8), (1, 64)):
         for par in (0, 1):
             for p in range(TILES):
-                row_out[0, d, par, p] = bar_e[par, p + 1, first : first + 8]
+                row_out[d, par, p] = bar_e[par, p + 1, first : first + 8]
     for s, (q, first_lane) in enumerate(((1, 0), (TILES, 112))):
         col_out[0, s] = packed(
             [bar_e[par, q, 8 + 16 * k : 24 + 16 * k] for par in (0, 1) for k in range(4)], first_lane, 16
@@ -142,6 +148,14 @@
 
     pl.semaphore_wait(barrier, sum(i.astype(jnp.int32) for i in inside))
     start_out(0)
+    for ref in (x_e, bar_e):
+        for par in (0, 1):
+            for q in range(TILES + 2):
+                if q in (0, TILES + 1):
+                    ref[par, q] = jnp.zeros((80, 128), F32)
+                else:
+                    ref[par, q, 0:8] = jnp.zeros((8, 128), F32)
+                    ref[par, q, 72:80] = jnp.zeros((8, 128), F32)
 
     for load in loads[TILES : TILES + 2]:
         load.wait()
@@ -191,13 +205,16 @@
     for p in range(TILES):
         weights_t[p * T_ROWS + 64 : p * T_ROWS + 128, 0:128] = jnp.zeros((64, 128), BF16)
 
+    nothing = jnp.zeros((32, 128), BF16)
+
     def build(q, carry):
         for p in range(TILES):
             for r in range(4):
                 line = base_v[r, pl.ds(q * 8 + p, 1), :]
-                rolled = pltpu.roll(jnp.broadcast_to(line, (128, 128)), 0, 1, stride=1, stride_axis=0)
+                rolled = pltpu.roll(jnp.broadcast_to(line, (96, 128)), 0, 1, stride=1, stride_axis=0)
                 start = pl.multiple_of(p * 4096 + (q * 4 + r) * 128, 128)
-                weights[pl.ds(start, 128), :] = jnp.where(band, rolled, 0.0).astype(BF16)
+                weights[pl.ds(start, 96), :] = jnp.where(band[:96], rolled, 0.0).astype(BF16)
+                weights[pl.ds(start + 96, 32), :] = nothing
                 line = base_v[4 + r, pl.ds(q * 8 + p, 1), :]
                 rolled = pltpu.roll(jnp.broadcast_to(line, (64, 128)), 0, 1, stride=1, stride_axis=0).astype(BF16)
                 for d in (0, 1):
@@ -254,7 +271,8 @@
 
     def blur_own(p, carry):
         lhs = stacked_rows(shifted, p, ((0, 0, PAIRS), (1, 0, PAIRS)))
-        matrix = weights[pl.ds(pl.multiple_of(p * 4096, 4096), 4096), :]
+        start = p * 4096 if isinstance(p, int) else pl.multiple_of(p * 4096, 4096)
+        matrix = weights[pl.ds(start, 4096), :]
         blur_v[p] = jnp.dot(lhs, matrix, preferred_element_type=F32)
         return carry
 
@@ -278,17 +296,19 @@
         q1_v[par, p, a:b] = u1 / shrink
         q2_v[par, p, a:b] = u2 / shrink
 
-    def merged(par, q, a, b):
-        lane = lanes((b - a, 128))
-        if q == 0:
-            value = spread[par, 0, 0, a:b] + jnp.where(lane >= 64, roll(spread[par, 1, 0, a:b], 64), 0.0)
-        elif q == TILES:
-            value = jnp.where(lane < 64, roll(spread[par, 1, q - 1, a:b], 64), 0.0)
-        else:
-            value = spread[par, 0, q, a:b] + jnp.where(
-                lane >= 64, roll(spread[par, 1, q, a:b], 64), roll(spread[par, 1, q - 1, a:b], 64)
-            )
-        return roll(value, 113)
+    def moved_tiles(par, a, b, wanted):
+        firsts = [roll(spread[par, 0, p, a:b], 113) if wanted(p - 1) or wanted(p) else None for p in range(TILES)]
+        seconds = [roll(spread[par, 1, p, a:b], 49) if wanted(p) or wanted(p + 1) else None for p in range(TILES)]
+        return firsts + [0.0], [0.0] + seconds
+
+    def merged(p, tiles, rows_count):
+        firsts, seconds = tiles
+        lane = lanes((rows_count, 128))
+        if p == -1:
+            return jnp.where(lane >= 113, firsts[0], 0.0)
+        if p == TILES:
+            return jnp.where(lane < 15, seconds[TILES], 0.0)
+        return jnp.where(lane < 113, firsts[p], firsts[p + 1]) + jnp.where(lane >= 49, seconds[p + 1], seconds[p])
 
     def own_part(par, p, a, b, tiles):
         lane = lanes((b - a, 128))
@@ -307,22 +327,20 @@
         before = jnp.where(lane == 0, outer, roll(m2, 1))
         if p + 1 == TILES:
             m2 = jnp.where((lane == 127) & right, 0.0, m2)
-        return jnp.where(lane < 113, tiles[p], tiles[p + 1]) - ((m1 - above) + (m2 - before))
+        return merged(p, tiles, b - a) - ((m1 - above) + (m2 - before))
 
     def rim_part(par, p, d, tiles):
-        value = jnp.where(lane8 < 113, tiles[p], tiles[p + 1])
+        value = merged(p, tiles, 8)
         if d == 1 and par == 0:
             edge = jnp.concatenate([q1_v[1, p, PAIRS - 1 : PAIRS], jnp.zeros((7, 128), F32)], axis=0)
             value = value + edge
         return value
 
-    def side_part(par, s, a, b, tile):
-        lane = lanes((b - a, 128))
-        if s == 0:
-            return jnp.where(lane >= 113, tile, 0.0)
-        value = jnp.where(lane < 15, tile, 0.0)
-        if 8 <= a < 72:
-            value = value + jnp.where(lane == 0, roll(q2_v[par, TILES - 1, a - 8 : b - 8], 1), 0.0)
+    def side_part(par, s, a, b, tiles):
+        value = merged(TILES if s else -1, tiles, b - a)
+        if s == 1 and 8 <= a < 72:
+            edge = roll(q2_v[par, TILES - 1, a - 8 : b - 8], 1)
+            value = value + jnp.where(lanes((b - a, 128)) == 0, edge, 0.0)
         return value
 
     def masked(direction, value):
@@ -385,15 +403,17 @@
                 spread[1, h, p, 0:80] = out[80 * h : 80 * h + 80, 0:128]
                 spread[0, h, p, 1:81] = out[80 * h : 80 * h + 80, 128:256]
 
-        extras = [blur_halo(p) for p in range(TILES)]
-        for p in range(TILES):
+        order = (0, 1, 2, 3)
+        extras = {p: blur_halo(p) for p in order}
+        for p in order:
             dual(p, extras[p])
-        for p in range(TILES):
+        for p in (0, 1, 2, 3):
             adjoint(p)
 
     for par in (0, 1):
         lay(shifted, par, 8, 72)
-    lax.fori_loop(0, TILES, blur_own, 0)
+    for p in range(TILES):
+        blur_own(p, 0)
     for p in range(TILES - 1):
         tv(0, p, 0, PAIRS)
         tv(1, p, 0, PAIRS - 8)
@@ -402,7 +422,7 @@
     for par in (0, 1):
         for d, (a, b) in ((0, (0, 8)), (1, (72, 80))):
             for p in range(TILES):
-                value = masked(d, row_in[0, d, par, p])
+                value = masked(d, row_in[d, par, p])
                 x_e[par, p + 1, a:b] = value
                 bar_e[par, p + 1, a:b] = value
             for s, q in ((0, 0), (1, TILES + 1)):
@@ -424,29 +444,33 @@
     for par in (0, 1):
         tv(par, TILES - 1, 0, PAIRS)
 
+    every = lambda p: True
     for par in (0, 1):
         for d, first in ((0, 0), (1, 64)):
+            strip = [[], [], [], []]
             for a, b in ((first, first + 8), (first + 8, first + 16)):
                 own = 8 <= a < 72
-                tiles = [merged(par, q, a, b) for q in range(TILES + 1)]
+                tiles = moved_tiles(par, a, b, every)
                 for p in range(TILES):
                     value = own_part(par, p, a, b, tiles) if own else rim_part(par, p, d, tiles)
                     acc[par, p + 1, a:b] = value
-                    wide_row_out[d, TILES * par + p, a - first : b - first] = value
-                acc[par, 0, a:b] = side_part(par, 0, a, b, tiles[0])
-                acc[par, TILES + 1, a:b] = side_part(par, 1, a, b, tiles[TILES])
+                    strip[p].append(value)
+                acc[par, 0, a:b] = side_part(par, 0, a, b, tiles)
+                acc[par, TILES + 1, a:b] = side_part(par, 1, a, b, tiles)
+            for p in range(TILES):
+                wide_row_out[d, TILES * par + p] = jnp.concatenate(strip[p], axis=0).astype(STRIP_TYPE)
         a, b = 16, 64
-        tiles = [merged(par, q, a, b) if q != 2 else None for q in range(TILES + 1)]
+        tiles = moved_tiles(par, a, b, lambda p: p not in (1, 2))
         for p in (0, TILES - 1):
             acc[par, p + 1, a:b] = own_part(par, p, a, b, tiles)
-        acc[par, 0, a:b] = side_part(par, 0, a, b, tiles[0])
-        acc[par, TILES + 1, a:b] = side_part(par, 1, a, b, tiles[TILES])
+        acc[par, 0, a:b] = side_part(par, 0, a, b, tiles)
+        acc[par, TILES + 1, a:b] = side_part(par, 1, a, b, tiles)
     for d, first in ((0, 0), (1, 64)):
         message = None
         for f, (par, s) in enumerate(((0, 0), (0, 1), (1, 0), (1, 1))):
             moved = roll(acc[par, (TILES + 1) * s, first : first + 16], 16 * f - 112 + 112 * s)
             message = moved if f == 0 else jnp.where(lane16 >= 16 * f, moved, message)
-        wide_row_out[d, 2 * TILES] = message
+        wide_row_out[d, 2 * TILES] = message.astype(STRIP_TYPE)
     for s, q in ((0, 0), (1, TILES)):
         around = [
             jnp.where(lanes((80, 128)) < 16, roll(acc[par, q], 16), roll(acc[par, q + 1], 16)) for par in (0, 1)
@@ -467,7 +491,7 @@
 
     for par in (0, 1):
         a, b = 16, 64
-        tiles = [None] + [merged(par, q, a, b) for q in (1, 2, 3)] + [None]
+        tiles = moved_tiles(par, a, b, lambda p: p in (1, 2))
         for p in range(TILES):
             value = own_part(par, p, a, b, tiles) if p in (1, 2) else acc[par, p + 1, a:b]
             old = x_e[par, p + 1, a:b]
@@ -488,6 +512,7 @@
         tv(1, p, 8, 48)
 
     wait_in(1)
+    strips = [[wide_row_in[d, i].astype(F32) for i in range(2 * TILES + 1)] for d in (0, 1)]
     for par in (0, 1):
         beside = []
         for s in (0, 1):
@@ -514,11 +539,11 @@
                 for q in range(TILES + 2):
                     value = acc[par, q, a:b]
                     if 1 <= q <= TILES:
-                        value = value + masked(d, wide_row_in[d, TILES * par + q - 1, 8 * k8 : 8 * k8 + 8])
+                        value = value + masked(d, strips[d][TILES * par + q - 1][8 * k8 : 8 * k8 + 8])
                     else:
                         s = 0 if q == 0 else 1
                         f = 2 * par + s
-                        more = roll(wide_row_in[d, 2 * TILES, 8 * k8 : 8 * k8 + 8], 112 - 112 * s - 16 * f)
+                        more = roll(strips[d][2 * TILES][8 * k8 : 8 * k8 + 8], 112 - 112 * s - 16 * f)
                         value = value + masked(d, jnp.where((lane8 >= 112) if s == 0 else (lane8 < 16), more, 0.0))
                     for s, line in ((0, 0), (1, TILES)):
                         if q in (line, line + 1):
@@ -555,27 +580,35 @@
             tv(par, p, 0, PAIRS)
 
     corners = [[None, None] for _ in range(4)]
+    strip = [[[], [], [], []] for _ in (0, 1)]
     for par in (0, 1):
         for d, (a, b) in ((0, (0, 8)), (1, (72, 80))):
-            tiles = [merged(par, q, a, b) for q in range(TILES + 1)]
+            tiles = moved_tiles(par, a, b, every)
             for p in range(TILES):
-                row_out[1, d, par, p] = rim_part(par, p, d, tiles)
+                strip[d][p].append(rim_part(par, p, d, tiles))
             for s in (0, 1):
-                corners[2 * d + s][par] = side_part(par, s, a, b, tiles[TILES * s])
+                corners[2 * d + s][par] = side_part(par, s, a, b, tiles)
+    for d in (0, 1):
+        for p in range(TILES):
+            last_row_out[d, p] = jnp.concatenate(strip[d][p], axis=0)
     for s, first_lane in ((0, 112), (1, 0)):
-        side = [side_part(par, s, 8, 72, merged(par, TILES * s, 8, 72)) for par in (0, 1)]
+        side = [
+            side_part(par, s, 8, 72, moved_tiles(par, 8, 72, lambda p: p == (TILES if s else -1)))
+            for par in (0, 1)
+        ]
         col_out[1, s] = packed([side[par][16 * k : 16 * k + 16] for par in (0, 1) for k in range(4)], first_lane, 16)
         for d in (0, 1):
             cor_out[1, 2 * d + s] = packed(corners[2 * d + s], first_lane, 8)
     start_out(2)
 
     for par in (0, 1):
-        tiles = [merged(par, q, 8, 72) for q in range(TILES + 1)]
+        tiles = moved_tiles(par, 8, 72, every)
         for p in range(TILES):
             x_e[par, p + 1, 8:72] = x_e[par, p + 1, 8:72] - TAU * own_part(par, p, 8, 72, tiles)
             dual_out_ref[p, pl.ds(par, PAIRS, stride=2), :] = y_v[par, p]
 
     wait_in(2)
+    strips = [[last_row_in[d, p] for p in range(TILES)] for d in (0, 1)]
 
     def subtract(par, q, a, b, value):
         x_e[par, q, a:b] = x_e[par, q, a:b] - TAU * value
@@ -589,7 +622,7 @@
                 subtract(par, q, 8 + 16 * k, 24 + 16 * k, value)
         for d, (a, b) in ((0, (8, 16)), (1, (64, 72))):
             for p in range(TILES):
-                value = masked(d, row_in[1, d, par, p])
+                value = masked(d, strips[d][p][8 * par : 8 * par + 8])
                 if p in (0, TILES - 1):
                     s = 0 if p == 0 else 1
                     message = masked(4 + 2 * d + s, cor_in[1, 2 * d + s])
@@ -649,18 +682,20 @@
             pltpu.VMEM((TILES, 128, 128), F32),
             pltpu.VMEM((2, TILES, 96, 128), F32),
             pltpu.VMEM((2, 2, TILES, 88, 128), F32),
-            pltpu.VMEM((2, 2, 2, TILES, 8, 128), F32),
+            pltpu.VMEM((2, 2, TILES, 8, 128), F32),
             pltpu.VMEM((2, 2, 16, 128), F32),
             pltpu.VMEM((2, 4, 8, 128), F32),
-            pltpu.VMEM((2, 2, 2, TILES, 8, 128), F32),
+            pltpu.VMEM((2, 2, TILES, 8, 128), F32),
             pltpu.VMEM((2, 2, 16, 128), F32),
             pltpu.VMEM((2, 4, 8, 128), F32),
-            pltpu.VMEM((2, 2 * TILES + 1, 16, 128), F32),
+            pltpu.VMEM((2, 2 * TILES + 1, 16, 128), STRIP_TYPE),
             pltpu.VMEM((2, 40, 128), F32),
             pltpu.VMEM((4, 8, 128), F32),
-            pltpu.VMEM((2, 2 * TILES + 1, 16, 128), F32),
+            pltpu.VMEM((2, 2 * TILES + 1, 16, 128), STRIP_TYPE),
             pltpu.VMEM((2, 40, 128), F32),
             pltpu.VMEM((4, 8, 128), F32),
+            pltpu.VMEM((2, TILES, 16, 128), F32),
+            pltpu.VMEM((2, TILES, 16, 128), F32),
             pltpu.SemaphoreType.DMA((4 * TILES + 2,)),
             pltpu.SemaphoreType.DMA((EXCHANGES, 8)),
             pltpu.SemaphoreType.DMA((EXCHANGES, 8)),

time: 24.7 us -> 23.7 us (0.960)
  Pallas kernels: 23.8 us -> 22.9 us
    pallas_call x1, Pallas kernels: 23 us -> 22.1 us  [per_device(): pl.pallas_call(kernel, out_shape=(pltpu.VMEM(tiled, F32), pltpu.VMEM(tile...]
where the time goes in v5:
time: 23.7 us; the launch traced here: 23.5 us
  Pallas kernels  22.9 us (97%)
  between operations  0.64 us (3%)
    pallas_call x1, Pallas kernels, per_device(): pl.pallas_call(kernel, out_shape=(pltpu.VMEM(tiled, F32), pltpu.VMEM(tile...  22.1 us
    pallas_call x1, Pallas kernels, per_device(): pl.pallas_call(put_out, out_shape=(jax.ShapeDtypeStruct(shape, F32), jax....  0.85 us

profile of v5, /device:TPU:27, one launch (start us, length us, event | category | flops | bytes accessed | tf_op | source)
XLA Modules:
  0.0 23.5 jit_solution(4900647597192072685)
XLA Ops:
  0.6 22.1 %shard_map.77 = (f32[4,128,128]{2,1,0:T(8,128)S(1)}, f32[4,128,128]{2,1,0:T(8,128)S(1)}) custom-call(s32[1,4]{1,0:T(1,128)} %index_hbm.1, f32[128,512]{1,0:T(8,128)} %observed_hbm.1, bf16[31,31,64]{2,1,0:T(8,128)(2,1)} %bitcast.1, f32[128,512]{1,0:T(8,128)} %start_hbm.1, f32[128,512]{1,0:T(8,128)} %dual_hbm.1, f32[2,128,512]{2,1,0:T(8,128)} %tv_hbm.1), custom_call_target="tpu_custom_call" | custom-call | tf_op jit(solution)/shard_map/pallas_call | solution.py:658
  22.7 0.9 %shard_map.78 = (f32[128,512]{1,0:T(8,128)}, f32[128,512]{1,0:T(8,128)}) custom-call(f32[4,128,128]{2,1,0:T(8,128)S(1)} %get-tuple-element.4.restored_ref, f32[4,128,128]{2,1,0:T(8,128)S(1)} %get-tuple-element.5.dual_ref), custom_call_target="tpu_custom_call" | custom-call | tf_op jit(solution)/shard_map/pallas_call | solution.py:705

commit v6 on v5

--- a/solution.py
+++ b/solution.py
@@ -29,6 +29,7 @@
     return value if shift == 0 else pltpu.roll(value, shift, 1)
 
 
+W_ROWS = 32 * 96
 T_ROWS = 17 * 128
 
 
@@ -205,16 +206,14 @@
     for p in range(TILES):
         weights_t[p * T_ROWS + 64 : p * T_ROWS + 128, 0:128] = jnp.zeros((64, 128), BF16)
 
-    nothing = jnp.zeros((32, 128), BF16)
 
     def build(q, carry):
         for p in range(TILES):
             for r in range(4):
                 line = base_v[r, pl.ds(q * 8 + p, 1), :]
                 rolled = pltpu.roll(jnp.broadcast_to(line, (96, 128)), 0, 1, stride=1, stride_axis=0)
-                start = pl.multiple_of(p * 4096 + (q * 4 + r) * 128, 128)
+                start = pl.multiple_of(p * W_ROWS + (q * 4 + r) * 96, 32)
                 weights[pl.ds(start, 96), :] = jnp.where(band[:96], rolled, 0.0).astype(BF16)
-                weights[pl.ds(start + 96, 32), :] = nothing
                 line = base_v[4 + r, pl.ds(q * 8 + p, 1), :]
                 rolled = pltpu.roll(jnp.broadcast_to(line, (64, 128)), 0, 1, stride=1, stride_axis=0).astype(BF16)
                 for d in (0, 1):
@@ -243,36 +242,53 @@
 
     def stacked_rows(source, p, ranges):
         pieces = []
-        for t in range(16):
-            for par in (1, 0):
-                first = t + 1 - par
-                pieces.append(
-                    jnp.concatenate(
-                        [source[par, h, p, a + first : a + first + n] for h, a, n in ranges], axis=0
-                    ).astype(BF16)
-                )
+        for t in range(0, 16, 2):
+            parts = []
+            for v in (0, 1):
+                for par in (1, 0):
+                    first = t + v + 1 - par
+                    parts.append(
+                        jnp.concatenate(
+                            [source[par, v, h, p, a + first : a + first + n] for h, a, n in ranges], axis=0
+                        )
+                    )
+            lane = lanes(parts[0].shape)
+            for i, border in enumerate((96, 64, 32)):
+                pieces.append(jnp.where(lane < border, parts[i], parts[i + 1]).astype(BF16))
         return jnp.concatenate(pieces, axis=1)
+
+    def starts_at(par, v):
+        return (96 - 64 * v if par == 0 else 64 * v)
+
+    def beyond(lane, offset, k):
+        return ((lane - offset) & 127) >= k
 
     def lay(target, par, a, b):
         lane = lanes((b - a, 128))
         tiles = [bar_e[par, q, a:b] for q in range(TILES + 2)]
-        by15 = [roll(t, 15) for t in tiles[:-1]]
-        by79 = [roll(t, 79) for t in tiles[1:]]
-        for p in range(TILES):
-            target[par, 0, p, a:b] = jnp.where(lane < 15, by15[p], by15[p + 1])
-            target[par, 1, p, a:b] = jnp.where(lane < 79, by79[p], by79[p + 1])
+        for v in (0, 1):
+            offset = starts_at(par, v)
+            by15 = [roll(t, 15 + offset) for t in tiles[:-1]]
+            by79 = [roll(t, 79 + offset) for t in tiles[1:]]
+            for p in range(TILES):
+                target[par, v, 0, p, a:b] = jnp.where(beyond(lane, offset, 15), by15[p + 1], by15[p])
+                target[par, v, 1, p, a:b] = jnp.where(beyond(lane, offset, 79), by79[p + 1], by79[p])
 
     def lay_sides(par, a, b, reach_in):
         lane = lanes((b - a, 128))
-        first = jnp.where(lane < 15, roll(bar_e[par, 0, a:b], 15), roll(bar_e[par, 1, a:b], 15))
-        last = jnp.where(lane < 79, roll(bar_e[par, TILES, a:b], 79), roll(bar_e[par, TILES + 1, a:b], 79))
-        shifted_halo[par, 0, 0, a:b] = jnp.where(lane < 15 + reach_in, first, 0.0)
-        shifted_halo[par, 1, TILES - 1, a:b] = jnp.where(lane >= 79 - reach_in, last, 0.0)
+        for v in (0, 1):
+            offset = starts_at(par, v)
+            outer, inner = roll(bar_e[par, 0, a:b], 15 + offset), roll(bar_e[par, 1, a:b], 15 + offset)
+            first = jnp.where(beyond(lane, offset, 15), inner, outer)
+            inner, outer = roll(bar_e[par, TILES, a:b], 79 + offset), roll(bar_e[par, TILES + 1, a:b], 79 + offset)
+            last = jnp.where(beyond(lane, offset, 79), outer, inner)
+            shifted_halo[par, v, 0, 0, a:b] = jnp.where(beyond(lane, offset, 15 + reach_in), 0.0, first)
+            shifted_halo[par, v, 1, TILES - 1, a:b] = jnp.where(beyond(lane, offset, 79 - reach_in), last, 0.0)
 
     def blur_own(p, carry):
         lhs = stacked_rows(shifted, p, ((0, 0, PAIRS), (1, 0, PAIRS)))
-        start = p * 4096 if isinstance(p, int) else pl.multiple_of(p * 4096, 4096)
-        matrix = weights[pl.ds(start, 4096), :]
+        start = p * W_ROWS if isinstance(p, int) else pl.multiple_of(p * W_ROWS, W_ROWS)
+        matrix = weights[pl.ds(start, W_ROWS), :]
         blur_v[p] = jnp.dot(lhs, matrix, preferred_element_type=F32)
         return carry
 
@@ -360,7 +376,7 @@
                     ranges += [(h, 0, edge), (h, PAIRS - edge, edge)]
             return jnp.dot(
                 stacked_rows(shifted_halo, p, ranges),
-                weights[p * 4096 : p * 4096 + 4096],
+                weights[p * W_ROWS : p * W_ROWS + W_ROWS],
                 preferred_element_type=F32,
             )
 
@@ -403,11 +419,11 @@
                 spread[1, h, p, 0:80] = out[80 * h : 80 * h + 80, 0:128]
                 spread[0, h, p, 1:81] = out[80 * h : 80 * h + 80, 128:256]
 
-        order = (0, 1, 2, 3)
+        order = (0, 1, 3, 2)
         extras = {p: blur_halo(p) for p in order}
         for p in order:
             dual(p, extras[p])
-        for p in (0, 1, 2, 3):
+        for p in order:
             adjoint(p)
 
     for par in (0, 1):
@@ -500,12 +516,15 @@
             bar_e[par, p + 1, a:b] = 2.0 * new - old
         lay(shifted, par, a, b)
         lane = lanes((b - a, 128))
-        shifted[par, 0, 0, a:b] = jnp.where(lane < 30, 0.0, shifted[par, 0, 0, a:b])
-        shifted[par, 1, TILES - 1, a:b] = jnp.where(lane >= 64, 0.0, shifted[par, 1, TILES - 1, a:b])
-        for h in (0, 1):
-            for p in range(TILES):
-                shifted[par, h, p, 8:16] = jnp.zeros((8, 128), F32)
-                shifted[par, h, p, 64:72] = jnp.zeros((8, 128), F32)
+        for v in (0, 1):
+            offset = starts_at(par, v)
+            first, last = shifted[par, v, 0, 0, a:b], shifted[par, v, 1, TILES - 1, a:b]
+            shifted[par, v, 0, 0, a:b] = jnp.where(beyond(lane, offset, 30), first, 0.0)
+            shifted[par, v, 1, TILES - 1, a:b] = jnp.where(beyond(lane, offset, 64), 0.0, last)
+            for h in (0, 1):
+                for p in range(TILES):
+                    shifted[par, v, h, p, 8:16] = jnp.zeros((8, 128), F32)
+                    shifted[par, v, h, p, 64:72] = jnp.zeros((8, 128), F32)
     lax.fori_loop(0, TILES, blur_own, 0)
     for p in (1, 2):
         tv(0, p, 8, 56)
@@ -668,7 +687,7 @@
             pltpu.VMEM(tiled, F32),
             pltpu.VMEM((2,) + tiled, F32),
             pltpu.VMEM((8, 64, 128), F32),
-            pltpu.VMEM((TILES * 4096, 128), BF16),
+            pltpu.VMEM((TILES * W_ROWS, 128), BF16),
             pltpu.VMEM((TILES * T_ROWS, 256), BF16),
             pltpu.VMEM(extended, F32),
             pltpu.VMEM(extended, F32),
@@ -677,8 +696,8 @@
             pltpu.VMEM(block, F32),
             pltpu.VMEM(block, F32),
             pltpu.VMEM(block, F32),
-            pltpu.VMEM((2, 2, TILES, 80, 128), F32),
-            pltpu.VMEM((2, 2, TILES, 80, 128), F32),
+            pltpu.VMEM((2, 2, 2, TILES, 80, 128), F32),
+            pltpu.VMEM((2, 2, 2, TILES, 80, 128), F32),
             pltpu.VMEM((TILES, 128, 128), F32),
             pltpu.VMEM((2, TILES, 96, 128), F32),
             pltpu.VMEM((2, 2, TILES, 88, 128), F32),

time: 23.7 us -> 23.6 us (level)
  no operation moved by 1% of the time
where the time goes in v6:
time: 23.6 us; the launch traced here: 23.5 us
  Pallas kernels  22.8 us (97%)
  between operations  0.64 us (3%)
    pallas_call x1, Pallas kernels, per_device(): pl.pallas_call(kernel, out_shape=(pltpu.VMEM(tiled, F32), pltpu.VMEM(tile...  22 us
    pallas_call x1, Pallas kernels, per_device(): pl.pallas_call(put_out, out_shape=(jax.ShapeDtypeStruct(shape, F32), jax....  0.85 us

profile of v6, /device:TPU:27, one launch (start us, length us, event | category | flops | bytes accessed | tf_op | source)
XLA Modules:
  0.0 23.5 jit_solution(14885500813046697841)
XLA Ops:
  0.6 22.0 %shard_map.77 = (f32[4,128,128]{2,1,0:T(8,128)S(1)}, f32[4,128,128]{2,1,0:T(8,128)S(1)}) custom-call(s32[1,4]{1,0:T(1,128)} %index_hbm.1, f32[128,512]{1,0:T(8,128)} %observed_hbm.1, bf16[31,31,64]{2,1,0:T(8,128)(2,1)} %bitcast.1, f32[128,512]{1,0:T(8,128)} %start_hbm.1, f32[128,512]{1,0:T(8,128)} %dual_hbm.1, f32[2,128,512]{2,1,0:T(8,128)} %tv_hbm.1), custom_call_target="tpu_custom_call" | custom-call | tf_op jit(solution)/shard_map/pallas_call | solution.py:677
  22.6 0.9 %shard_map.78 = (f32[128,512]{1,0:T(8,128)}, f32[128,512]{1,0:T(8,128)}) custom-call(f32[4,128,128]{2,1,0:T(8,128)S(1)} %get-tuple-element.4.restored_ref, f32[4,128,128]{2,1,0:T(8,128)S(1)} %get-tuple-element.5.dual_ref), custom_call_target="tpu_custom_call" | custom-call | tf_op jit(solution)/shard_map/pallas_call | solution.py:724
